TPU v7x, 128 devices: a whole 4x4x4 slice. The times are simulated.
128 devices in a mesh: zone: 8 (over x, y_lo), dev: 16 (over y_hi, z, core).
Axes of the slice: x: 4, y: 4 (y_hi: 2, y_lo: 2; y = y_hi * 2 + y_lo), z: 4, core: 2. Of those that a mesh axis runs over, the one named last changes fastest.
Arguments:
- node_features: bfloat16 [65536, 512], P(('zone', 'dev')), may hold values from -9 to 9
- neighbour_blocks: int32 [512, 32], P(('zone', 'dev')), may hold values from 0 to 511, as said below
- neighbour_count: int32 [512], P(('zone', 'dev')), may hold values from 8 to 32, as said below
- tile_valid: int32 [512], replicated, may hold values from 64 to 128
- w_query: bfloat16 [512, 512], replicated, may hold values from -0.5 to 0.5
- w_key: bfloat16 [512, 512], replicated, may hold values from -0.5 to 0.5
- w_value: bfloat16 [512, 512], replicated, may hold values from -0.25 to 0.25
- w_out: bfloat16 [512, 512], replicated, may hold values from -0.25 to 0.25
- w_gate: bfloat16 [512, 2048], replicated, may hold values from -0.25 to 0.25
- w_up: bfloat16 [512, 2048], replicated, may hold values from -0.25 to 0.25
- w_down: bfloat16 [2048, 512], replicated, may hold values from -0.125 to 0.125
Outputs:
- layer_out: bfloat16 [65536, 512], P(('zone', 'dev'))
Inputs may be any that keep to these rules, and one draw needn't show every extreme that they name: `neighbour_blocks`: each row lists 32 different blocks. Zones are runs of 64 blocks (zone of block g is g // 64); every listed block lies in the query block's zone or in one of the two zones beside it, counting around the last zone to the first. Each value is 8, 16 or 32, one value for each patch of 16 consecutive blocks (patch of block g is g // 16); only the first neighbour_count[b] slots of row b count.
All inputs are finite; a program needn't handle non-finite values.
Results may differ from a plain program's by a relative error of at most 0.007.
The roundings to bfloat16 on the way count: a program that leaves them out, or rounds other values in their place, can miss the bound.
Values may be sent and summed in bfloat16 or wider, within the bound.
A program may use at most 448 MiB of HBM per device.

v0:
```python
import functools
import math

import jax
import jax.numpy as jnp
from jax import lax
from jax.experimental import pallas as pl
from jax.experimental.pallas import tpu as pltpu
from jax.sharding import PartitionSpec as P

D = 512
HEADS = 4
HD = 128
TILE = 128
NB = 32
ZD = 4
NEG = -1e30
EXP_SCALE = math.log2(math.e) / math.sqrt(HD)


def proj_kernel(x_ref, wq_ref, wk_ref, wv_ref, q_ref, kv_ref):
    def one_tile(t, carry):
        x = x_ref[pl.ds(pl.multiple_of(t * TILE, TILE), TILE), :]
        q = jnp.dot(x, wq_ref[...], preferred_element_type=jnp.float32).astype(jnp.bfloat16)
        for h in range(HEADS):
            q_ref[h, t] = q[:, h * HD:(h + 1) * HD]
        k = jnp.dot(x, wk_ref[...], preferred_element_type=jnp.float32)
        for h in range(HEADS):
            kv_ref[h, t, 0] = jnp.transpose(k[:, h * HD:(h + 1) * HD]).astype(jnp.bfloat16)
        v = jnp.dot(x, wv_ref[...], preferred_element_type=jnp.float32).astype(jnp.bfloat16)
        for h in range(HEADS):
            kv_ref[h, t, 1] = v[:, h * HD:(h + 1) * HD]
        return carry

    lax.fori_loop(0, x_ref.shape[0] // TILE, one_tile, 0)


def project(x, wq, wk, wv):
    tiles = x.shape[0] // TILE
    return pl.pallas_call(
        proj_kernel,
        out_shape=(
            jax.ShapeDtypeStruct((HEADS, tiles, TILE, HD), jnp.bfloat16),
            jax.ShapeDtypeStruct((HEADS, tiles, 2, TILE, HD), jnp.bfloat16),
        ),
    )(x, wq, wk, wv)


MESH = pl.DeviceIdType.MESH
DIRECT = 3
UP_SET = (0, 2)
DOWN_SET = (1, 3)


def exchange_kernel(code_ref, q_ref, kv_ref, code_out, q_out, kv_out, transit, send_sem, recv_sem):
    zone, dev = lax.axis_index("zone"), lax.axis_index("dev")
    x, y_lo = zone // 2, zone % 2
    y_hi, z, core = dev // 8, (dev // 2) % ZD, dev % 2
    y = y_hi * 2 + y_lo

    def at(px, py, pz, pc):
        return (px * 2 + py % 2, (py // 2) * 8 + pz * 2 + pc)

    side = 1 - 2 * y_lo
    up, down = at(x, (y + 1) % 4, z, core), at(x, (y + 3) % 4, z, core)
    halo, back = at((x + 4 + side) % 4, y, z, core), at((x + 4 - side) % 4, y, z, core)
    partner = at(x, y, z, 1 - core)
    z_at = [z] + [(z + d) % ZD for d in (1, 3, 2)]
    z_dev = [None] + [at(x, y, z_at[j], core) for j in (1, 2, 3)]

    barrier = pltpu.get_barrier_semaphore()
    peers = [up, down, halo, back, partner] + z_dev[1:]
    for peer in peers:
        pl.semaphore_signal(barrier, inc=1, device_id=peer, device_id_type=MESH)
    pl.semaphore_wait(barrier, len(peers))

    live = []

    def send(src, dst, target):
        k = len(live)
        copy = pltpu.make_async_remote_copy(
            src_ref=src,
            dst_ref=dst,
            send_sem=send_sem.at[k],
            recv_sem=recv_sem.at[k],
            device_id=target,
            device_id_type=MESH,
        )
        copy.start()
        live.append(copy)
        return copy

    def place(slot, j):
        return kv_out.at[slot, core, z_at[j]]

    kv_z, q_z, code_z, shared = {}, {}, {}, []
    for j, lands in ((1, 2), (2, 1), (3, 3)):
        kv_z[lands] = send(kv_ref.at[z_at[j]], kv_out.at[0, core, z], z_dev[j])
    kv_out[0, core, z] = kv_ref[z]
    q_out[z] = q_ref[z]
    code_out[z] = code_ref[...]

    from_up, from_down, far, halo_up, halo_down = {}, {}, {}, {}, {}

    def spread_own(j, src):
        from_down[j] = send(src, place(2, j), up)
        from_up[j] = send(src, place(1, j), down)
        if j == DIRECT:
            from_down["x"] = send(src, transit, back)
        shared.append(send(src, place(0, j), partner))

    def pass_on(j):
        from_up[j].wait_recv()
        if j in DOWN_SET:
            far[j] = send(place(1, j), place(3, j), down)
        if j != DIRECT:
            halo_up[j] = send(place(1, j), place(4, j), halo)
        shared.append(send(place(1, j), place(1, j), partner))
        from_down[j].wait_recv()
        if j in UP_SET:
            far[j] = send(place(2, j), place(3, j), up)
        if j != DIRECT:
            halo_down[j] = send(place(2, j), place(5, j), halo)
        shared.append(send(place(2, j), place(2, j), partner))

    spread_own(0, kv_ref.at[z])
    for j, lands in ((1, 2), (2, 1), (3, 3)):
        q_z[lands] = send(q_ref.at[z_at[j]], q_out.at[z], z_dev[j])
        code_z[lands] = send(code_ref, code_out.at[z], z_dev[j])
    for j in (1, 2):
        kv_z[j].wait_recv()
        spread_own(j, place(0, j))
    pass_on(0)
    kv_z[3].wait_recv()
    spread_own(3, place(0, 3))
    pass_on(1)
    pass_on(2)
    from_down["x"].wait_recv()
    halo_down[DIRECT] = send(transit, place(5, DIRECT), up)
    halo_up[DIRECT] = send(transit, place(4, DIRECT), down)
    pass_on(3)
    for j in range(4):
        far[j].wait_recv()
        shared.append(send(place(3, j), place(3, j), partner))
        halo_up[j].wait_recv()
        shared.append(send(place(4, j), place(4, j), partner))
        halo_down[j].wait_recv()
        shared.append(send(place(5, j), place(5, j), partner))
    for c in shared + list(q_z.values()) + list(code_z.values()):
        c.wait_recv()
    for c in live:
        c.wait_send()


COPIES = 3 + 6 + 2 * 4 + 1 + 4 + 4 + 6 + 2 + 8 + 12


def exchange(code, q, kv):
    tiles = kv.shape[1]
    piece = kv.shape[1:]
    return pl.pallas_call(
        exchange_kernel,
        out_shape=(
            jax.ShapeDtypeStruct((ZD,) + code.shape, jnp.int32),
            jax.ShapeDtypeStruct(q.shape, q.dtype),
            jax.ShapeDtypeStruct((6, 2, ZD) + piece, kv.dtype),
        ),
        in_specs=[pl.BlockSpec(memory_space=pltpu.VMEM)] * 3,
        out_specs=[pl.BlockSpec(memory_space=pltpu.VMEM)] * 3,
        scratch_shapes=[
            pltpu.VMEM(piece, kv.dtype),
            pltpu.SemaphoreType.DMA((COPIES,)),
            pltpu.SemaphoreType.DMA((COPIES,)),
        ],
        compiler_params=pltpu.CompilerParams(
            collective_id=0, has_side_effects=True, vmem_limit_bytes=24 * 1024 * 1024
        ),
    )(code, q, kv)


LEAD = 5


def attn_kernel(code_ref, q_ref, kv_ref, o_ref, s_even, s_odd, top_ref, den_ref, acc_ref):
    tiles = q_ref.shape[0]
    lane = lax.broadcasted_iota(jnp.int32, (1, TILE), 1)
    rings = (s_even, s_odd)

    def groups(i):
        return code_ref[i, NB] // 8

    def advance(i, c):
        last = c + 1 >= groups(i)
        return jnp.where(last, jnp.minimum(i + 1, tiles), i), jnp.where(last, 0, c + 1)

    def scores(i, c, ring, slot):
        q = q_ref[jnp.minimum(i, tiles - 1)]
        top = jnp.where(c == 0, NEG, top_ref[i])
        for p in range(4):
            a = code_ref[i, c * 8 + 2 * p]
            b = code_ref[i, c * 8 + 2 * p + 1]
            keys = jnp.concatenate([kv_ref[a // 256, 0], kv_ref[b // 256, 0]], axis=1)
            s = jnp.dot(q, keys, preferred_element_type=jnp.float32)
            bias = jnp.concatenate(
                [jnp.where(lane < a % 256, 0.0, NEG), jnp.where(lane < b % 256, 0.0, NEG)],
                axis=1,
            )
            s = s + bias
            ring[slot, :, p * 256:(p + 1) * 256] = s
            top = jnp.maximum(top, jnp.maximum(s[:, :TILE], s[:, TILE:]))
        top_ref[i] = top

    def values(i, c, peak, ring, slot):
        den = jnp.where(c == 0, 0.0, den_ref[...])
        acc = jnp.where(c == 0, 0.0, acc_ref[...])
        ps, vs = [], []
        for p in range(4):
            a = code_ref[i, c * 8 + 2 * p]
            b = code_ref[i, c * 8 + 2 * p + 1]
            w = jnp.exp2((ring[slot, :, p * 256:(p + 1) * 256] - peak) * EXP_SCALE)
            den = den + (w[:, :TILE] + w[:, TILE:])
            ps.append(w.astype(jnp.bfloat16))
            vs += [kv_ref[a // 256, 1], kv_ref[b // 256, 1]]
        acc = acc + jnp.dot(
            jnp.concatenate(ps, axis=1),
            jnp.concatenate(vs, axis=0),
            preferred_element_type=jnp.float32,
        )
        den_ref[...] = den
        acc_ref[...] = acc
        o_ref[i] = (acc / jnp.sum(den, axis=1, keepdims=True)).astype(jnp.bfloat16)

    total = lax.fori_loop(0, tiles, lambda i, n: n + groups(i), 0)
    head = (jnp.int32(0), jnp.int32(0))
    for w in range(LEAD):
        scores(*head, rings[w % 2], w // 2)
        head = advance(*head)

    def pair(k, state):
        head, tail = state
        tails = (tail, advance(*tail))
        peaks = [jnp.max(top_ref[i], axis=1, keepdims=True) for i, _ in tails]
        for r in range(2):
            w = 2 * k + r
            scores(*head, rings[(r + LEAD) % 2], ((w + LEAD) // 2) % 4)
            values(*tails[r], peaks[r], rings[r], (w // 2) % 4)
            head = advance(*head)
        return head, advance(*tails[1])

    lax.fori_loop(0, (total + 1) // 2, pair, (head, (jnp.int32(0), jnp.int32(0))))


def attend(code, q, kv):
    tiles = q.shape[0]
    ring = pltpu.VMEM((4, TILE, 8 * TILE), jnp.float32)
    square = pltpu.VMEM((TILE, TILE), jnp.float32)
    return pl.pallas_call(
        attn_kernel,
        out_shape=jax.ShapeDtypeStruct((tiles + 1,) + q.shape[1:], jnp.bfloat16),
        in_specs=[
            pl.BlockSpec(memory_space=pltpu.SMEM),
            pl.BlockSpec(memory_space=pltpu.VMEM),
            pl.BlockSpec(memory_space=pltpu.VMEM),
        ],
        out_specs=pl.BlockSpec(memory_space=pltpu.VMEM),
        scratch_shapes=[
            ring, ring, pltpu.VMEM((tiles + 1, TILE, TILE), jnp.float32), square, square
        ],
        compiler_params=pltpu.CompilerParams(vmem_limit_bytes=24 * 1024 * 1024),
    )(code, q, kv)


def finish_kernel(
    o_ref, x_hbm, wo_hbm, wg_hbm, wu_hbm, wd_hbm, out_ref,
    x_ref, wo_ref, wg_ref, wu_ref, wd_ref, got, res_ref, norm_ref, hid_ref,
    load_sem, send_sem, recv_sem,
):
    dev = lax.axis_index("dev")
    zone = lax.axis_index("zone")
    z = (dev // 2) % ZD
    tiles = x_ref.shape[0] // TILE
    z_at = [(z + d) % ZD for d in (1, 3, 2)]
    peers = [(zone, dev + 2 * (pz - z)) for pz in z_at]

    barrier = pltpu.get_barrier_semaphore()
    for peer in peers:
        pl.semaphore_signal(barrier, inc=1, device_id=peer, device_id_type=MESH)
    loads = [
        pltpu.make_async_copy(src, dst, load_sem.at[i])
        for i, (src, dst) in enumerate(
            (
                (x_hbm, x_ref), (wo_hbm, wo_ref), (wg_hbm, wg_ref), (wu_hbm, wu_ref), (wd_hbm, wd_ref)
            )
        )
    ]
    for c in loads:
        c.start()
    pl.semaphore_wait(barrier, len(peers))
    copies = {}
    for k, lands in ((2, 2), (0, 1), (1, 0)):
        copies[lands] = pltpu.make_async_remote_copy(
            src_ref=o_ref.at[pl.ds(z_at[k] * tiles, tiles)],
            dst_ref=got.at[lands],
            send_sem=send_sem.at[lands],
            recv_sem=recv_sem.at[lands],
            device_id=peers[k],
            device_id_type=MESH,
        )
        copies[lands].start()

    def add_head(head, piece):
        o = piece.reshape(tiles * TILE, HD)
        w = wo_ref[pl.ds(pl.multiple_of(head * HD, HD), HD), :]
        return jnp.dot(o, w, preferred_element_type=jnp.float32)

    loads[0].wait()
    loads[1].wait()
    res_ref[...] = x_ref[...].astype(jnp.float32) + add_head(
        z, o_ref[pl.ds(z * tiles, tiles)]
    )
    for k in (0, 1, 2):
        copies[k].wait_recv()
        res_ref[...] += add_head(z_at[k], got[k])
    r = res_ref[...]
    inverse = lax.rsqrt(jnp.mean(r * r, axis=-1, keepdims=True) + 1e-06)
    norm_ref[...] = (r * inverse).astype(jnp.bfloat16)
    loads[2].wait()
    loads[3].wait()
    width = 256

    def hidden(f, carry):
        cols = pl.ds(pl.multiple_of(f * width, width), width)
        gate = jnp.dot(norm_ref[...], wg_ref[:, cols], preferred_element_type=jnp.float32)
        up = jnp.dot(norm_ref[...], wu_ref[:, cols], preferred_element_type=jnp.float32)
        hid_ref[:, cols] = (gate / (1.0 + jnp.exp(-gate)) * up).astype(jnp.bfloat16)
        return carry

    lax.fori_loop(0, wg_ref.shape[1] // width, hidden, 0)
    loads[4].wait()

    def down(f, carry):
        cols = pl.ds(pl.multiple_of(f * width, width), width)
        out_ref[:, cols] = (
            res_ref[:, cols]
            + jnp.dot(hid_ref[...], wd_ref[:, cols], preferred_element_type=jnp.float32)
        ).astype(jnp.bfloat16)
        return carry

    lax.fori_loop(0, D // width, down, 0)
    for c in copies.values():
        c.wait_send()


def finish_layer(o, x, w_out, w_gate, w_up, w_down):
    rows = x.shape[0]
    tiles = rows // TILE
    ff = w_gate.shape[1]
    return pl.pallas_call(
        finish_kernel,
        out_shape=jax.ShapeDtypeStruct(x.shape, x.dtype),
        in_specs=[pl.BlockSpec(memory_space=pltpu.VMEM)]
        + [pl.BlockSpec(memory_space=pl.ANY)] * 5,
        out_specs=pl.BlockSpec(memory_space=pltpu.VMEM),
        scratch_shapes=[
            pltpu.VMEM(x.shape, x.dtype),
            pltpu.VMEM(w_out.shape, w_out.dtype),
            pltpu.VMEM(w_gate.shape, w_gate.dtype),
            pltpu.VMEM(w_up.shape, w_up.dtype),
            pltpu.VMEM(w_down.shape, w_down.dtype),
            pltpu.VMEM((ZD - 1, tiles, TILE, HD), jnp.bfloat16),
            pltpu.VMEM(x.shape, jnp.float32),
            pltpu.VMEM(x.shape, jnp.bfloat16),
            pltpu.VMEM((rows, ff), jnp.bfloat16),
            pltpu.SemaphoreType.DMA((5,)),
            pltpu.SemaphoreType.DMA((ZD - 1,)),
            pltpu.SemaphoreType.DMA((ZD - 1,)),
        ],
        compiler_params=pltpu.CompilerParams(
            collective_id=1, has_side_effects=True, vmem_limit_bytes=24 * 1024 * 1024
        ),
    )(o, x, w_out, w_gate, w_up, w_down)


def make_codes(neighbour_blocks, neighbour_count, tile_valid, zone_blocks, zone_count):
    zone = lax.axis_index("zone")
    y_lo = zone % 2
    y = (lax.axis_index("dev") // 8) * 2 + y_lo
    relative = (neighbour_blocks // zone_blocks - zone + 1) % zone_count
    local = neighbour_blocks % zone_blocks
    y_hi, rest = local // 32, local % 32
    z, rest = rest // 8, rest % 8
    core, t = rest // 4, rest % 4
    other_y = y_hi * 2 + 1 - y_lo
    above = (other_y - y + 4) % 4 == 1
    same_x = relative == 2 - 2 * y_lo
    near = jnp.where(same_x, jnp.where(above, 1, 2), jnp.where(above, 4, 5))
    slot = jnp.where(relative == 1, jnp.where(y_hi == y // 2, 0, 3), near)
    place = ((slot * 2 + core) * ZD + z) * 4 + t
    matches = neighbour_blocks[..., None] == jnp.arange(tile_valid.shape[0], dtype=jnp.int32)
    valid = jnp.sum(jnp.where(matches, tile_valid, 0), axis=-1)
    live = jnp.arange(NB, dtype=jnp.int32)[None, :] < neighbour_count[:, None]
    code = place * 256 + jnp.where(live, valid, 0)
    code = jnp.concatenate(
        [code, neighbour_count[:, None], jnp.zeros((code.shape[0], 95), jnp.int32)], axis=1
    )
    return jnp.concatenate([code, jnp.zeros_like(code)], axis=0)


def body(
    x,
    neighbour_blocks,
    neighbour_count,
    tile_valid,
    w_query,
    w_key,
    w_value,
    w_out,
    w_gate,
    w_up,
    w_down,
):
    rows = x.shape[0]
    tiles = rows // TILE
    zone_count = lax.axis_size("zone")
    dev_count = lax.axis_size("dev")
    codes = make_codes(
        neighbour_blocks, neighbour_count, tile_valid, tiles * dev_count, zone_count
    )
    q, kv = project(x, w_query, w_key, w_value)
    codes, q, kv = exchange(codes, q, kv)
    o = attend(
        jnp.pad(codes[:, :tiles].reshape(ZD * tiles, -1), ((0, 8), (0, 0))),
        q.reshape(ZD * tiles, TILE, HD),
        kv.reshape(6 * 2 * ZD * tiles, 2, TILE, HD),
    )
    return finish_layer(o, x, w_out, w_gate, w_up, w_down)


def solution(mesh):
    placed = (
        P(("zone", "dev"), None),
        P(("zone", "dev"), None),
        P(("zone", "dev")),
        P(),
        P(),
        P(),
        P(),
        P(),
        P(),
        P(),
        P(),
    )
    return jax.shard_map(
        body, mesh=mesh, in_specs=placed, out_specs=P(("zone", "dev"), None), check_vma=False
    )
```

profile of v0, /device:TPU:14, one launch (start us, length us, event | category | flops | bytes accessed | tf_op | source)
XLA Modules:
  0.0 98.3 jit_solution(16570527293299878825)
XLA Ops:
  0.0 0.1 pad.8.clone
  0.1 0.9 select_reduce_fusion
  1.0 0.8 select_add_fusion
  1.8 0.7 copy.13
  2.5 0.1 add_add_fusion
  2.6 4.0 %shard_map.109 = (bf16[4,4,128,128]{3,2,1,0:T(8,128)(2,1)}, bf16[4,4,2,128,128]{4,3,2,1,0:T(8,128)(2,1)}) custom-call(bf16[512,512]{1,0:T(8,128)(2,1)} %x_hbm.1, bf16[512,512]{1,0:T(8,128)(2,1)} %wq_ref.1, bf16[512,512]{1,0:T(8,128)(2,1)} %wk_ref.1, bf16[512,512]{1,0:T(8,128)(2,1)} %wv_ref.1), custom_call_target="tpu_custom_call" | custom-call | tf_op jit(solution)/shard_map/pallas_call | solution.py:40
  6.6 0.0 copy-start.4
  6.6 1.2 %copy-done.4 = bf16[4,4,2,128,128]{4,3,2,1,0:T(8,128)(2,1)S(1)} copy-done((bf16[4,4,2,128,128]{4,3,2,1,0:T(8,128)(2,1)S(1)}, bf16[4,4,2,128,128]{4,3,2,1,0:T(8,128)(2,1)}, u32[]{:S(2)}) %copy-start.4) | copy-done | bytes 1048600
  7.9 0.0 copy-start.6
  7.9 1.0 %copy-done.6 = bf16[4,4,128,128]{3,2,1,0:T(8,128)(2,1)S(1)} copy-done((bf16[4,4,128,128]{3,2,1,0:T(8,128)(2,1)S(1)}, bf16[4,4,128,128]{3,2,1,0:T(8,128)(2,1)}, u32[]{:S(2)}) %copy-start.6) | copy-done | bytes 524312
  8.9 50.2 %shard_map.110 = (s32[4,8,128]{2,1,0:T(8,128)S(1)}, bf16[4,4,128,128]{3,2,1,0:T(8,128)(2,1)S(1)}, bf16[6,2,4,4,2,128,128]{6,5,4,3,2,1,0:T(8,128)(2,1)S(1)}) custom-call(s32[8,128]{1,0:T(8,128)S(1)} %concatenate.7.code_ref, bf16[4,4,128,128]{3,2,1,0:T(8,128)(2,1)S(1)} %copy-done.6, bf16[4,4,2,128,128]{4,3,2,1,0:T(8,128)(2,1)S(1)} %copy-done.4), custom_call_target="tpu_custom_call" | custom-call | tf_op jit(solution)/shard_map/pallas_call | solution.py:161
  59.2 0.0 copy-start
  59.2 0.0 copy-start.1
  59.2 0.0 copy-start.2
  59.2 0.0 copy-start.3
  59.2 0.0 copy-start.5
  59.2 22.3 %shard_map.111.o_ref = bf16[17,128,128]{2,1,0:T(8,128)(2,1)S(1)} custom-call(s32[24,128]{1,0:T(8,128)S(1)} %pad.5.code_ref, bf16[16,128,128]{2,1,0:T(8,128)(2,1)S(1)} %bitcast.5, bf16[192,2,128,128]{3,2,1,0:T(8,128)(2,1)S(1)} %bitcast.4), custom_call_target="tpu_custom_call" | custom-call | tf_op jit(solution)/shard_map/pallas_call | solution.py:257
  81.6 0.0 copy-done
  81.6 0.0 copy-done.1
  81.6 0.0 copy-done.2
  81.6 0.0 copy-done.3
  81.6 0.0 copy-done.5
  81.6 15.8 %shard_map.112 = bf16[512,512]{1,0:T(8,128)(2,1)S(1)} custom-call(bf16[17,128,128]{2,1,0:T(8,128)(2,1)S(1)} %shard_map.111.o_ref, bf16[512,512]{1,0:T(8,128)(2,1)S(1)} %copy-done, bf16[512,512]{1,0:T(8,128)(2,1)S(1)} %copy-done.5, bf16[512,2048]{1,0:T(8,128)(2,1)S(1)} %copy-done.1, bf16[512,2048]{1,0:T(8,128)(2,1)S(1)} %copy-done.2, ...), custom_call_target="tpu_custom_call" | custom-call | tf_op jit(solution)/shard_map/pallas_call | solution.py:358
  97.5 0.8 copy.15
  (4 shorter events, 0.0 us)
Async XLA Ops:
  6.6 1.2 %copy-start.4 = (bf16[4,4,2,128,128]{4,3,2,1,0:T(8,128)(2,1)S(1)}, bf16[4,4,2,128,128]{4,3,2,1,0:T(8,128)(2,1)}, u32[]{:S(2)}) copy-start(bf16[4,4,2,128,128]{4,3,2,1,0:T(8,128)(2,1)} %get-tuple-element.11.kv_ref) | copy-start | bytes 3145732
  7.9 1.0 %copy-start.6 = (bf16[4,4,128,128]{3,2,1,0:T(8,128)(2,1)S(1)}, bf16[4,4,128,128]{3,2,1,0:T(8,128)(2,1)}, u32[]{:S(2)}) copy-start(bf16[4,4,128,128]{3,2,1,0:T(8,128)(2,1)} %get-tuple-element.10.q_ref) | copy-start | bytes 1572868
  59.2 22.4 %copy-start = (bf16[512,512]{1,0:T(8,128)(2,1)S(1)}, bf16[512,512]{1,0:T(8,128)(2,1)}, u32[]{:S(2)}) copy-start(bf16[512,512]{1,0:T(8,128)(2,1)} %x_hbm.1) | copy-start | bytes 1572868
  59.2 22.4 %copy-start.1 = (bf16[512,2048]{1,0:T(8,128)(2,1)S(1)}, bf16[512,2048]{1,0:T(8,128)(2,1)}, u32[]{:S(2)}) copy-start(bf16[512,2048]{1,0:T(8,128)(2,1)} %wg_hbm.1) | copy-start | bytes 6291460
  59.2 22.4 %copy-start.2 = (bf16[512,2048]{1,0:T(8,128)(2,1)S(1)}, bf16[512,2048]{1,0:T(8,128)(2,1)}, u32[]{:S(2)}) copy-start(bf16[512,2048]{1,0:T(8,128)(2,1)} %wu_hbm.1) | copy-start | bytes 6291460
  59.2 22.4 %copy-start.3 = (bf16[2048,512]{1,0:T(8,128)(2,1)S(1)}, bf16[2048,512]{1,0:T(8,128)(2,1)}, u32[]{:S(2)}) copy-start(bf16[2048,512]{1,0:T(8,128)(2,1)} %wd_hbm.1) | copy-start | bytes 6291460
  59.2 22.4 %copy-start.5 = (bf16[512,512]{1,0:T(8,128)(2,1)S(1)}, bf16[512,512]{1,0:T(8,128)(2,1)}, u32[]{:S(2)}) copy-start(bf16[512,512]{1,0:T(8,128)(2,1)} %wo_hbm.1) | copy-start | bytes 1572868
where the time goes:
time: 99.1 us; the launch traced here: 98.3 us
  Pallas kernels  92.5 us (93%)
  local copies, waits for them, and re-layouts  3.93 us (4%)
  other arithmetic  1.76 us (2%)
    pallas_call x1, Pallas kernels, exchange(): pl.pallas_call(exchange_kernel, out_shape=(jax.ShapeDtypeStruct((ZD,) + c...  50.2 us
    pallas_call x1, Pallas kernels, attend(): pl.pallas_call(attn_kernel, out_shape=jax.ShapeDtypeStruct((tiles + 1,) +...  22.3 us
    pallas_call x1, Pallas kernels, finish_layer(): pl.pallas_call(finish_kernel, out_shape=jax.ShapeDtypeStruct(x.shape, x.d...  15.8 us
    pallas_call x1, Pallas kernels, project(): pl.pallas_call(proj_kernel, out_shape=(jax.ShapeDtypeStruct((HEADS, tiles...  4.05 us
    unnamed x15, local copies, waits for them, and re-layouts  3.09 us

commit v1 on v0

v1 whole, which is shorter than its diff:
```python
import math

import jax
import jax.numpy as jnp
from jax import lax
from jax.experimental import pallas as pl
from jax.experimental.pallas import tpu as pltpu
from jax.sharding import PartitionSpec as P

D = 512
HEADS = 4
HD = 128
TILE = 128
NB = 32
ZD = 4
NEG = -1e30
EXP_SCALE = math.log2(math.e) / math.sqrt(HD)


MESH = pl.DeviceIdType.MESH
UNITS = tuple((j, h) for j in range(ZD) for h in range(2))
DIRECT = ((1, 0), (1, 1), (2, 1))
COPIES = 112


def exchange_kernel(
    nb_ref, count_ref, valid_ref, x_ref, wq_ref, wk_ref, wv_ref,
    code_out, q_out, kv_out,
    kv_ref, q_ref, raw, raw_all, relay, transit, send_sem, recv_sem,
):
    zone, dev = lax.axis_index("zone"), lax.axis_index("dev")
    x, y_lo = zone // 2, zone % 2
    y_hi, z, core = dev // 8, (dev // 2) % ZD, dev % 2
    y = y_hi * 2 + y_lo
    tiles = x_ref.shape[0] // TILE
    half = tiles // 2

    def at(px, py, pz, pc):
        return (px * 2 + py % 2, (py // 2) * 8 + pz * 2 + pc)

    side = 1 - 2 * y_lo
    up, down = at(x, (y + 1) % 4, z, core), at(x, (y + 3) % 4, z, core)
    halo, back = at((x + 4 + side) % 4, y, z, core), at((x + 4 - side) % 4, y, z, core)
    partner = at(x, y, z, 1 - core)
    z_at = [(z + d) % ZD for d in (0, 1, 3, 2)]
    z_dev = [at(x, y, pz, core) for pz in z_at]

    barrier = pltpu.get_barrier_semaphore()
    peers = [up, down, halo, back, partner] + z_dev[1:]
    for peer in peers:
        pl.semaphore_signal(barrier, inc=1, device_id=peer, device_id_type=MESH)

    lane = lax.broadcasted_iota(jnp.int32, (1, 128), 1)
    raw[...] = jnp.full(raw.shape, -1, jnp.int32)
    raw[:tiles, :NB] = nb_ref[...]
    for t in range(tiles):
        n = count_ref[t]
        row = jnp.where(lane < jnp.minimum(n, NB), raw[t:t + 1, :], -1)
        raw[t:t + 1, :] = jnp.where(lane == NB, n, row)

    def rows_of(t):
        return x_ref[pl.ds(pl.multiple_of(t * TILE, TILE), TILE), :]

    def keys_values(t, carry):
        rows = rows_of(t)
        k = jnp.dot(rows, wk_ref[...], preferred_element_type=jnp.float32)
        for h in range(HEADS):
            kv_ref[h, t, 0] = jnp.transpose(k[:, h * HD:(h + 1) * HD]).astype(jnp.bfloat16)
        v = jnp.dot(rows, wv_ref[...], preferred_element_type=jnp.float32).astype(jnp.bfloat16)
        for h in range(HEADS):
            kv_ref[h, t, 1] = v[:, h * HD:(h + 1) * HD]
        return carry

    lax.fori_loop(0, tiles, keys_values, 0)
    kv_out[0, core, z] = kv_ref[z]
    pl.semaphore_wait(barrier, len(peers))

    live, shared = [], []

    def send(source, target, device):
        k = len(live)
        copy = pltpu.make_async_remote_copy(
            src_ref=source,
            dst_ref=target,
            send_sem=send_sem.at[k],
            recv_sem=recv_sem.at[k],
            device_id=device,
            device_id_type=MESH,
        )
        copy.start()
        live.append(copy)
        return copy

    def part(h):
        return pl.ds(h * half, half)

    def place(slot, u):
        return kv_out.at[slot, core, z_at[u[0]], part(u[1])]

    def share(slot, u, source=None):
        shared.append(send(place(slot, u) if source is None else source, place(slot, u), partner))

    own, relayed, q_in, raw_in = {}, {}, {}, {}
    above, below, far, halo_above, halo_below, passing = {}, {}, {}, {}, {}, {}

    def send_z(h):
        own[2, h] = send(kv_ref.at[z_at[1], part(h)], kv_out.at[0, core, z, part(h)], z_dev[1])
        own[1, h] = send(kv_ref.at[z_at[2], part(h)], kv_out.at[0, core, z, part(h)], z_dev[2])

    def spread(u, source):
        below[u] = send(source, place(2, u), up)
        above[u] = send(source, place(1, u), down)

    def straight(u):
        passing[u] = send(place(0, u), transit.at[DIRECT.index(u)], back)

    def cross(u):
        passing[u].wait_recv()
        spot = transit.at[DIRECT.index(u)]
        halo_below[u] = send(spot, place(5, u), up)
        halo_above[u] = send(spot, place(4, u), down)

    def arrived(u, fresh=True):
        above[u].wait_recv()
        if u[1] == 1:
            far[u] = send(place(1, u), place(3, u), down)
        if fresh:
            halo_above[u] = send(place(1, u), place(4, u), halo)
        share(1, u)
        below[u].wait_recv()
        if u[1] == 0:
            far[u] = send(place(2, u), place(3, u), up)
        if fresh:
            halo_below[u] = send(place(2, u), place(5, u), halo)
        share(2, u)

    def returned(u):
        halo_above[u].wait_recv()
        above[u] = send(place(4, u), place(1, u), back)
        share(4, u)
        halo_below[u].wait_recv()
        below[u] = send(place(5, u), place(2, u), back)
        share(5, u)

    def settle(u):
        halo_above[u].wait_recv()
        share(4, u)
        halo_below[u].wait_recv()
        share(5, u)

    def settle_far(u):
        far[u].wait_recv()
        share(3, u)

    def mine(u):
        own[u].wait_recv()
        share(0, u)

    send_z(0)
    spread((0, 0), kv_ref.at[z, part(0)])
    relayed[0] = send(kv_ref.at[z_at[3], part(0)], relay.at[0], z_dev[1])
    relayed[1] = send(kv_ref.at[z_at[3], part(1)], relay.at[1], z_dev[2])
    spread((0, 1), kv_ref.at[z, part(1)])
    send_z(1)
    share(0, (0, 0), kv_ref.at[z, part(0)])
    share(0, (0, 1), kv_ref.at[z, part(1)])

    def queries(t, carry):
        q = jnp.dot(rows_of(t), wq_ref[...], preferred_element_type=jnp.float32)
        q = q.astype(jnp.bfloat16)
        for h in range(HEADS):
            q_ref[h, t] = q[:, h * HD:(h + 1) * HD]
        return carry

    lax.fori_loop(0, tiles, queries, 0)
    q_out[z] = q_ref[z]
    raw_all[z] = raw[...]

    mine((1, 0))
    straight((1, 0))
    mine((2, 0))
    spread((2, 0), place(0, (2, 0)))
    relayed[0].wait_recv()
    own[3, 0] = send(relay.at[0], kv_out.at[0, core, z_at[2], part(0)], z_dev[1])
    relayed[1].wait_recv()
    own[3, 1] = send(relay.at[1], kv_out.at[0, core, z_at[1], part(1)], z_dev[2])
    for j, lands in ((1, 2), (2, 1), (3, 3)):
        raw_in[lands] = send(raw, raw_all.at[z], z_dev[j])
        q_in[lands] = send(q_ref.at[z_at[j]], q_out.at[z], z_dev[j])
    arrived((0, 0))
    arrived((0, 1))
    cross((1, 0))
    mine((1, 1))
    straight((1, 1))
    mine((2, 1))
    straight((2, 1))
    arrived((2, 0))
    mine((3, 0))
    spread((3, 0), place(0, (3, 0)))
    mine((3, 1))
    spread((3, 1), place(0, (3, 1)))
    returned((1, 0))
    settle_far((0, 0))
    settle((0, 0))
    cross((1, 1))
    cross((2, 1))
    arrived((3, 0))
    arrived((3, 1))
    arrived((1, 0), fresh=False)
    settle_far((0, 1))
    settle((0, 1))
    returned((1, 1))
    returned((2, 1))

    for j in (1, 2, 3):
        raw_in[j].wait_recv()
    lists = raw_all[...].reshape(ZD * raw.shape[0], 128)

    def look_up(i, found):
        return jnp.where(lists == i, valid_ref[i], found)

    found = lax.fori_loop(0, valid_ref.shape[0], look_up, jnp.zeros_like(lists))
    spot = jnp.maximum(lists, 0)
    relative = (spot // 64 + 9 - zone) % 8
    there_y = (spot // 32) % 2 * 2 + 1 - y_lo
    near = jnp.where((there_y + 4 - y) % 4 == 1, 1, 2)
    near = near + jnp.where(relative == 2 - 2 * y_lo, 0, 3)
    slot = jnp.where(relative == 1, jnp.where((spot // 32) % 2 == y_hi, 0, 3), near)
    code = ((slot * 2 + (spot // 4) % 2) * ZD + (spot // 8) % ZD) * 4 + spot % 4
    code = jnp.where(lists < 0, 0, code * 256 + found)
    code = jnp.where(lane == NB, lists, code)
    code_out[...] = jnp.zeros(code_out.shape, jnp.int32)
    for p in range(ZD):
        code_out[p * tiles:(p + 1) * tiles, :] = code[p * raw.shape[0]:p * raw.shape[0] + tiles]

    settle_far((2, 0))
    settle((2, 0))
    arrived((1, 1), fresh=False)
    arrived((2, 1), fresh=False)
    settle_far((1, 0))
    settle((3, 0))
    settle_far((3, 0))
    settle((3, 1))
    settle_far((3, 1))
    settle_far((1, 1))
    settle_far((2, 1))
    for c in shared + list(q_in.values()):
        c.wait_recv()
    for c in live:
        c.wait_send()


def exchange(lists, counts, valid, x, wq, wk, wv):
    tiles = x.shape[0] // TILE
    piece = (tiles, 2, TILE, HD)
    vmem, smem = pl.BlockSpec(memory_space=pltpu.VMEM), pl.BlockSpec(memory_space=pltpu.SMEM)
    return pl.pallas_call(
        exchange_kernel,
        out_shape=(
            jax.ShapeDtypeStruct((ZD * tiles + 8, 128), jnp.int32),
            jax.ShapeDtypeStruct((ZD, tiles, TILE, HD), x.dtype),
            jax.ShapeDtypeStruct((6, 2, ZD) + piece, x.dtype),
        ),
        in_specs=[vmem, smem, smem, vmem, vmem, vmem, vmem],
        out_specs=[vmem] * 3,
        scratch_shapes=[
            pltpu.VMEM((HEADS,) + piece, x.dtype),
            pltpu.VMEM((HEADS, tiles, TILE, HD), x.dtype),
            pltpu.VMEM((8, 128), jnp.int32),
            pltpu.VMEM((ZD, 8, 128), jnp.int32),
            pltpu.VMEM((2, tiles // 2) + piece[1:], x.dtype),
            pltpu.VMEM((len(DIRECT), tiles // 2) + piece[1:], x.dtype),
            pltpu.SemaphoreType.DMA((COPIES,)),
            pltpu.SemaphoreType.DMA((COPIES,)),
        ],
        compiler_params=pltpu.CompilerParams(
            collective_id=0, has_side_effects=True, vmem_limit_bytes=24 * 1024 * 1024
        ),
    )(lists, counts, valid, x, wq, wk, wv)


LEAD = 5


def attn_kernel(code_ref, q_ref, kv_ref, o_ref, s_even, s_odd, top_ref, den_ref, acc_ref):
    tiles = q_ref.shape[0]
    lane = lax.broadcasted_iota(jnp.int32, (1, TILE), 1)
    rings = (s_even, s_odd)

    def groups(i):
        return (code_ref[i, NB] + 7) // 8

    def advance(i, c):
        last = c + 1 >= groups(i)
        return jnp.where(last, jnp.minimum(i + 1, tiles), i), jnp.where(last, 0, c + 1)

    def scores(i, c, ring, slot):
        q = q_ref[jnp.minimum(i, tiles - 1)]
        top = jnp.where(c == 0, NEG, top_ref[i])
        for p in range(4):
            a = code_ref[i, c * 8 + 2 * p]
            b = code_ref[i, c * 8 + 2 * p + 1]
            keys = jnp.concatenate([kv_ref[a // 256, 0], kv_ref[b // 256, 0]], axis=1)
            s = jnp.dot(q, keys, preferred_element_type=jnp.float32)
            bias = jnp.concatenate(
                [jnp.where(lane < a % 256, 0.0, NEG), jnp.where(lane < b % 256, 0.0, NEG)],
                axis=1,
            )
            s = s + bias
            ring[slot, :, p * 256:(p + 1) * 256] = s
            top = jnp.maximum(top, jnp.maximum(s[:, :TILE], s[:, TILE:]))
        top_ref[i] = top

    def values(i, c, peak, ring, slot):
        den = jnp.where(c == 0, 0.0, den_ref[...])
        acc = jnp.where(c == 0, 0.0, acc_ref[...])
        ps, vs = [], []
        for p in range(4):
            a = code_ref[i, c * 8 + 2 * p]
            b = code_ref[i, c * 8 + 2 * p + 1]
            w = jnp.exp2((ring[slot, :, p * 256:(p + 1) * 256] - peak) * EXP_SCALE)
            den = den + (w[:, :TILE] + w[:, TILE:])
            ps.append(w.astype(jnp.bfloat16))
            vs += [kv_ref[a // 256, 1], kv_ref[b // 256, 1]]
        acc = acc + jnp.dot(
            jnp.concatenate(ps, axis=1),
            jnp.concatenate(vs, axis=0),
            preferred_element_type=jnp.float32,
        )
        den_ref[...] = den
        acc_ref[...] = acc
        o_ref[i] = (acc / jnp.sum(den, axis=1, keepdims=True)).astype(jnp.bfloat16)

    total = lax.fori_loop(0, tiles, lambda i, n: n + groups(i), 0)
    head = (jnp.int32(0), jnp.int32(0))
    for w in range(LEAD):
        scores(*head, rings[w % 2], w // 2)
        head = advance(*head)

    def pair(k, state):
        head, tail = state
        tails = (tail, advance(*tail))
        peaks = [jnp.max(top_ref[i], axis=1, keepdims=True) for i, _ in tails]
        for r in range(2):
            w = 2 * k + r
            scores(*head, rings[(r + LEAD) % 2], ((w + LEAD) // 2) % 4)
            values(*tails[r], peaks[r], rings[r], (w // 2) % 4)
            head = advance(*head)
        return head, advance(*tails[1])

    lax.fori_loop(0, (total + 1) // 2, pair, (head, (jnp.int32(0), jnp.int32(0))))


def attend(code, q, kv):
    tiles = q.shape[0]
    ring = pltpu.VMEM((4, TILE, 8 * TILE), jnp.float32)
    square = pltpu.VMEM((TILE, TILE), jnp.float32)
    return pl.pallas_call(
        attn_kernel,
        out_shape=jax.ShapeDtypeStruct((tiles + 1,) + q.shape[1:], jnp.bfloat16),
        in_specs=[
            pl.BlockSpec(memory_space=pltpu.SMEM),
            pl.BlockSpec(memory_space=pltpu.VMEM),
            pl.BlockSpec(memory_space=pltpu.VMEM),
        ],
        out_specs=pl.BlockSpec(memory_space=pltpu.VMEM),
        scratch_shapes=[
            ring, ring, pltpu.VMEM((tiles + 1, TILE, TILE), jnp.float32), square, square
        ],
        compiler_params=pltpu.CompilerParams(vmem_limit_bytes=24 * 1024 * 1024),
    )(code, q, kv)


def finish_kernel(
    o_ref, x_ref, wo_ref, wg_ref, wu_ref, wd_ref, out_ref,
    got, relay, res_ref, norm_ref, hid_ref, send_sem, recv_sem,
):
    zone, dev = lax.axis_index("zone"), lax.axis_index("dev")
    z = (dev // 2) % ZD
    tiles = x_ref.shape[0] // TILE
    half = tiles // 2
    z_at = [(z + d) % ZD for d in (1, 3, 2)]
    peers = [(zone, dev + 2 * (pz - z)) for pz in z_at[:2]]

    barrier = pltpu.get_barrier_semaphore()
    for peer in peers:
        pl.semaphore_signal(barrier, inc=1, device_id=peer, device_id_type=MESH)
    pl.semaphore_wait(barrier, len(peers))

    def send(k, source, target, device):
        copy = pltpu.make_async_remote_copy(
            src_ref=source,
            dst_ref=target,
            send_sem=send_sem.at[k],
            recv_sem=recv_sem.at[k],
            device_id=device,
            device_id_type=MESH,
        )
        copy.start()
        return copy

    hops = [
        send(h, o_ref.at[pl.ds(z_at[2] * tiles + h * half, half)], relay.at[h], peers[h])
        for h in range(2)
    ]
    ends = [
        send(2 + h, o_ref.at[pl.ds(z_at[h] * tiles, tiles)], got.at[1 - h], peers[h])
        for h in range(2)
    ]

    def add_head(head, piece):
        o = piece.reshape(tiles * TILE, HD)
        w = wo_ref[pl.ds(pl.multiple_of(head * HD, HD), HD), :]
        return jnp.dot(o, w, preferred_element_type=jnp.float32)

    res_ref[...] = x_ref[...].astype(jnp.float32) + add_head(
        z, o_ref[pl.ds(z * tiles, tiles)]
    )
    last = []
    for h in range(2):
        hops[h].wait_recv()
        last.append(send(4 + h, relay.at[h], got.at[2, pl.ds(h * half, half)], peers[h]))
    for h in range(2):
        ends[1 - h].wait_recv()
        res_ref[...] += add_head(z_at[h], got[h])
    for c in last:
        c.wait_recv()
    res_ref[...] += add_head(z_at[2], got[2])
    r = res_ref[...]
    inverse = lax.rsqrt(jnp.mean(r * r, axis=-1, keepdims=True) + 1e-06)
    norm_ref[...] = (r * inverse).astype(jnp.bfloat16)
    width = 256

    def hidden(f, carry):
        cols = pl.ds(pl.multiple_of(f * width, width), width)
        gate = jnp.dot(norm_ref[...], wg_ref[:, cols], preferred_element_type=jnp.float32)
        up = jnp.dot(norm_ref[...], wu_ref[:, cols], preferred_element_type=jnp.float32)
        hid_ref[:, cols] = (gate / (1.0 + jnp.exp(-gate)) * up).astype(jnp.bfloat16)
        return carry

    lax.fori_loop(0, wg_ref.shape[1] // width, hidden, 0)

    def down(f, carry):
        cols = pl.ds(pl.multiple_of(f * width, width), width)
        out_ref[:, cols] = (
            res_ref[:, cols]
            + jnp.dot(hid_ref[...], wd_ref[:, cols], preferred_element_type=jnp.float32)
        ).astype(jnp.bfloat16)
        return carry

    lax.fori_loop(0, D // width, down, 0)
    for c in hops + ends + last:
        c.wait_send()


def finish_layer(o, x, w_out, w_gate, w_up, w_down):
    rows = x.shape[0]
    tiles = rows // TILE
    ff = w_gate.shape[1]
    return pl.pallas_call(
        finish_kernel,
        out_shape=jax.ShapeDtypeStruct(x.shape, x.dtype),
        in_specs=[pl.BlockSpec(memory_space=pltpu.VMEM)] * 6,
        out_specs=pl.BlockSpec(memory_space=pltpu.VMEM),
        scratch_shapes=[
            pltpu.VMEM((ZD - 1, tiles, TILE, HD), jnp.bfloat16),
            pltpu.VMEM((2, tiles // 2, TILE, HD), jnp.bfloat16),
            pltpu.VMEM(x.shape, jnp.float32),
            pltpu.VMEM(x.shape, jnp.bfloat16),
            pltpu.VMEM((rows, ff), jnp.bfloat16),
            pltpu.SemaphoreType.DMA((6,)),
            pltpu.SemaphoreType.DMA((6,)),
        ],
        compiler_params=pltpu.CompilerParams(
            collective_id=1, has_side_effects=True, vmem_limit_bytes=24 * 1024 * 1024
        ),
    )(o, x, w_out, w_gate, w_up, w_down)


def body(
    x,
    neighbour_blocks,
    neighbour_count,
    tile_valid,
    w_query,
    w_key,
    w_value,
    w_out,
    w_gate,
    w_up,
    w_down,
):
    tiles = x.shape[0] // TILE
    codes, q, kv = exchange(
        neighbour_blocks, neighbour_count, tile_valid, x, w_query, w_key, w_value
    )
    o = attend(
        codes, q.reshape(ZD * tiles, TILE, HD), kv.reshape(6 * 2 * ZD * tiles, 2, TILE, HD)
    )
    return finish_layer(o, x, w_out, w_gate, w_up, w_down)


def solution(mesh):
    placed = (
        P(("zone", "dev"), None),
        P(("zone", "dev"), None),
        P(("zone", "dev")),
        P(),
        P(),
        P(),
        P(),
        P(),
        P(),
        P(),
        P(),
    )
    return jax.shard_map(
        body, mesh=mesh, in_specs=placed, out_specs=P(("zone", "dev"), None), check_vma=False
    )
```

time: 99.1 us -> 94.9 us (0.958)
  the two profiles are of different devices: /device:TPU:14 before, /device:TPU:8 now
where the time goes in v1:
time: 94.9 us; the launch traced here: 94.4 us
  Pallas kernels  87.3 us (92%)
  local copies, waits for them, and re-layouts  7.01 us (7%)
    pallas_call x1, Pallas kernels, exchange(): pl.pallas_call(exchange_kernel, out_shape=(jax.ShapeDtypeStruct((ZD * til...  49 us
    pallas_call x1, Pallas kernels, attend(): pl.pallas_call(attn_kernel, out_shape=jax.ShapeDtypeStruct((tiles + 1,) +...  22.4 us
    pallas_call x1, Pallas kernels, finish_layer(): pl.pallas_call(finish_kernel, out_shape=jax.ShapeDtypeStruct(x.shape, x.d...  15.8 us
    unnamed x25, local copies, waits for them, and re-layouts  7.01 us

profile of v1, /device:TPU:8, one launch (start us, length us, event | category | flops | bytes accessed | tf_op | source)
XLA Modules:
  0.0 94.4 jit_solution(10619308498732061136)
XLA Ops:
  0.0 0.0 copy-start
  0.0 1.0 %copy-done = bf16[512,512]{1,0:T(8,128)(2,1)S(1)} copy-done((bf16[512,512]{1,0:T(8,128)(2,1)S(1)}, bf16[512,512]{1,0:T(8,128)(2,1)}, u32[]{:S(2)}) %copy-start) | copy-done | bytes 524312
  1.0 0.0 copy-start.5
  1.0 1.0 %copy-done.5 = bf16[512,512]{1,0:T(8,128)(2,1)S(1)} copy-done((bf16[512,512]{1,0:T(8,128)(2,1)S(1)}, bf16[512,512]{1,0:T(8,128)(2,1)}, u32[]{:S(2)}) %copy-start.5) | copy-done | bytes 524312
  2.1 0.0 copy-start.6
  2.1 1.0 %copy-done.6 = bf16[512,512]{1,0:T(8,128)(2,1)S(1)} copy-done((bf16[512,512]{1,0:T(8,128)(2,1)S(1)}, bf16[512,512]{1,0:T(8,128)(2,1)}, u32[]{:S(2)}) %copy-start.6) | copy-done | bytes 524312
  3.1 0.0 copy-start.7
  3.1 1.0 %copy-done.7 = bf16[512,512]{1,0:T(8,128)(2,1)S(1)} copy-done((bf16[512,512]{1,0:T(8,128)(2,1)S(1)}, bf16[512,512]{1,0:T(8,128)(2,1)}, u32[]{:S(2)}) %copy-start.7) | copy-done | bytes 524312
  4.2 0.0 copy-start.9
  4.2 0.7 copy-done.9
  4.9 0.0 copy-start.10
  4.9 0.7 copy-done.10
  5.5 0.0 copy-start.11
  5.5 0.7 copy-done.11
  6.2 49.0 %shard_map.109 = (s32[24,128]{1,0:T(8,128)S(1)}, bf16[4,4,128,128]{3,2,1,0:T(8,128)(2,1)S(1)}, bf16[6,2,4,4,2,128,128]{6,5,4,3,2,1,0:T(8,128)(2,1)S(1)}) custom-call(s32[4,32]{1,0:T(4,128)S(1)} %copy-done.9, s32[4]{0:T(128)S(1)} %copy-done.11, s32[512]{0:T(512)S(1)} %copy-done.10, bf16[512,512]{1,0:T(8,128)(2,1)S(1)} %copy-done, ...), custom_call_target="tpu_custom_call" | custom-call | tf_op jit(solution)/shard_map/pallas_call | solution.py:257
  55.2 0.0 copy-start.1
  55.2 0.0 copy-start.2
  55.3 0.0 copy-start.3
  55.3 0.0 copy-start.4
  55.3 0.0 copy-start.8
  55.3 22.4 %shard_map.110.o_ref = bf16[17,128,128]{2,1,0:T(8,128)(2,1)S(1)} custom-call(s32[24,128]{1,0:T(8,128)S(1)} %get-tuple-element.8.code_ref, bf16[16,128,128]{2,1,0:T(8,128)(2,1)S(1)} %bitcast.3, bf16[192,2,128,128]{3,2,1,0:T(8,128)(2,1)S(1)} %bitcast.2), custom_call_target="tpu_custom_call" | custom-call | tf_op jit(solution)/shard_map/pallas_call | solution.py:358
  77.7 0.0 copy-done.1
  77.7 0.0 copy-done.2
  77.8 0.0 copy-done.3
  77.8 0.0 copy-done.4
  77.8 0.0 copy-done.8
  77.8 15.8 %shard_map.111 = bf16[512,512]{1,0:T(8,128)(2,1)S(1)} custom-call(bf16[17,128,128]{2,1,0:T(8,128)(2,1)S(1)} %shard_map.110.o_ref, bf16[512,512]{1,0:T(8,128)(2,1)S(1)} %copy-done.1, bf16[512,512]{1,0:T(8,128)(2,1)S(1)} %copy-done.8, bf16[512,2048]{1,0:T(8,128)(2,1)S(1)} %copy-done.2, bf16[512,2048]{1,0:T(8,128)(2,1)S(1)} %copy-done.3, ...), custom_call_target="tpu_custom_call" | custom-call | tf_op jit(solution)/shard_map/pallas_call | solution.py:460
  93.6 0.8 copy.13
Async XLA Ops:
  0.0 1.0 %copy-start = (bf16[512,512]{1,0:T(8,128)(2,1)S(1)}, bf16[512,512]{1,0:T(8,128)(2,1)}, u32[]{:S(2)}) copy-start(bf16[512,512]{1,0:T(8,128)(2,1)} %x_ref.3) | copy-start | bytes 1572868
  1.0 1.0 %copy-start.5 = (bf16[512,512]{1,0:T(8,128)(2,1)S(1)}, bf16[512,512]{1,0:T(8,128)(2,1)}, u32[]{:S(2)}) copy-start(bf16[512,512]{1,0:T(8,128)(2,1)} %wq_ref.1) | copy-start | bytes 1572868
  2.1 1.0 %copy-start.6 = (bf16[512,512]{1,0:T(8,128)(2,1)S(1)}, bf16[512,512]{1,0:T(8,128)(2,1)}, u32[]{:S(2)}) copy-start(bf16[512,512]{1,0:T(8,128)(2,1)} %wk_ref.1) | copy-start | bytes 1572868
  3.1 1.0 %copy-start.7 = (bf16[512,512]{1,0:T(8,128)(2,1)S(1)}, bf16[512,512]{1,0:T(8,128)(2,1)}, u32[]{:S(2)}) copy-start(bf16[512,512]{1,0:T(8,128)(2,1)} %wv_ref.1) | copy-start | bytes 1572868
  4.2 0.7 copy-start.9
  4.9 0.7 copy-start.10
  5.5 0.7 copy-start.11
  55.2 22.5 %copy-start.1 = (bf16[512,512]{1,0:T(8,128)(2,1)S(1)}, bf16[512,512]{1,0:T(8,128)(2,1)}, u32[]{:S(2)}) copy-start(bf16[512,512]{1,0:T(8,128)(2,1)} %x_ref.3) | copy-start | bytes 1572868
  55.2 22.5 %copy-start.2 = (bf16[512,2048]{1,0:T(8,128)(2,1)S(1)}, bf16[512,2048]{1,0:T(8,128)(2,1)}, u32[]{:S(2)}) copy-start(bf16[512,2048]{1,0:T(8,128)(2,1)} %wg_ref.1) | copy-start | bytes 6291460
  55.3 22.5 %copy-start.3 = (bf16[512,2048]{1,0:T(8,128)(2,1)S(1)}, bf16[512,2048]{1,0:T(8,128)(2,1)}, u32[]{:S(2)}) copy-start(bf16[512,2048]{1,0:T(8,128)(2,1)} %wu_ref.1) | copy-start | bytes 6291460
  55.3 22.5 %copy-start.4 = (bf16[2048,512]{1,0:T(8,128)(2,1)S(1)}, bf16[2048,512]{1,0:T(8,128)(2,1)}, u32[]{:S(2)}) copy-start(bf16[2048,512]{1,0:T(8,128)(2,1)} %wd_ref.1) | copy-start | bytes 6291460
  55.3 22.5 %copy-start.8 = (bf16[512,512]{1,0:T(8,128)(2,1)S(1)}, bf16[512,512]{1,0:T(8,128)(2,1)}, u32[]{:S(2)}) copy-start(bf16[512,512]{1,0:T(8,128)(2,1)} %wo_ref.1) | copy-start | bytes 1572868

commit v2 on v1

v2 whole, which is shorter than its diff:
```python
import math

import jax
import jax.numpy as jnp
from jax import lax
from jax.experimental import pallas as pl
from jax.experimental.pallas import tpu as pltpu
from jax.sharding import PartitionSpec as P

D = 512
HEADS = 4
HD = 128
TILE = 128
NB = 32
ZD = 4
NEG = -1e30
EXP_SCALE = math.log2(math.e) / math.sqrt(HD)


MESH = pl.DeviceIdType.MESH
UNITS = tuple((j, h) for j in range(ZD) for h in range(2))
DIRECT = ((1, 0), (1, 1), (2, 1))
COPIES = 112
ORDER = (3, 1, 2, 0)


def layer_kernel(
    nb_hbm, count_hbm, valid_hbm, x_hbm, wq_hbm, wk_hbm, wv_hbm, wo_hbm, wg_hbm, wu_hbm, wd_hbm,
    out_ref,
    nb_ref, count_ref, valid_ref, x_ref, wq_ref, wk_ref, wv_ref, wo_ref, wg_ref, wu_ref, wd_ref,
    kv_out, q_out, kv_ref, q_ref, raw, raw_all, relay, transit, code_vec, code_ref,
    s_even, s_odd, p_even, p_odd, d_even, d_odd, t_even, t_odd,
    o_ref, got, hop, res_ref, norm_ref, hid_ref,
    load_sem, send_sem, recv_sem,
):
    zone, dev = lax.axis_index("zone"), lax.axis_index("dev")
    x, y_lo = zone // 2, zone % 2
    y_hi, z, core = dev // 8, (dev // 2) % ZD, dev % 2
    y = y_hi * 2 + y_lo
    tiles = x_ref.shape[0] // TILE
    half = tiles // 2

    def at(px, py, pz, pc):
        return (px * 2 + py % 2, (py // 2) * 8 + pz * 2 + pc)

    side = 1 - 2 * y_lo
    up, down = at(x, (y + 1) % 4, z, core), at(x, (y + 3) % 4, z, core)
    halo, back = at((x + 4 + side) % 4, y, z, core), at((x + 4 - side) % 4, y, z, core)
    partner = at(x, y, z, 1 - core)
    z_at = [(z + d) % ZD for d in (0, 1, 3, 2)]
    z_dev = [at(x, y, pz, core) for pz in z_at]

    barrier = pltpu.get_barrier_semaphore()
    peers = [up, down, halo, back, partner] + z_dev[1:]
    for peer in peers:
        pl.semaphore_signal(barrier, inc=1, device_id=peer, device_id_type=MESH)

    loads = [
        pltpu.make_async_copy(source, target, load_sem.at[i])
        for i, (source, target) in enumerate(
            (
                (x_hbm, x_ref), (wk_hbm, wk_ref), (wv_hbm, wv_ref), (nb_hbm, nb_ref),
                (count_hbm, count_ref), (wq_hbm, wq_ref), (valid_hbm, valid_ref),
                (wo_hbm, wo_ref), (wg_hbm, wg_ref), (wu_hbm, wu_ref), (wd_hbm, wd_ref),
            )
        )
    ]
    for c in loads:
        c.start()
    for c in loads[:5]:
        c.wait()

    lane = lax.broadcasted_iota(jnp.int32, (1, 128), 1)
    raw[...] = jnp.full(raw.shape, -1, jnp.int32)
    raw[:tiles, :NB] = nb_ref[...]
    for t in range(tiles):
        n = count_ref[t]
        row = jnp.where(lane < jnp.minimum(n, NB), raw[t:t + 1, :], -1)
        raw[t:t + 1, :] = jnp.where(lane == NB, n, row)

    def rows_of(t):
        return x_ref[pl.ds(pl.multiple_of(t * TILE, TILE), TILE), :]

    def keys_values(t, carry):
        rows = rows_of(t)
        k = jnp.dot(rows, wk_ref[...], preferred_element_type=jnp.float32)
        for h in range(HEADS):
            kv_ref[h, t, 0] = jnp.transpose(k[:, h * HD:(h + 1) * HD]).astype(jnp.bfloat16)
        v = jnp.dot(rows, wv_ref[...], preferred_element_type=jnp.float32).astype(jnp.bfloat16)
        for h in range(HEADS):
            kv_ref[h, t, 1] = v[:, h * HD:(h + 1) * HD]
        return carry

    lax.fori_loop(0, tiles, keys_values, 0)
    kv_out[pl.ds((core * ZD + z) * tiles, tiles)] = kv_ref[z]
    pl.semaphore_wait(barrier, len(peers))

    live, shared = [], []

    def send(source, target, device):
        k = len(live)
        copy = pltpu.make_async_remote_copy(
            src_ref=source,
            dst_ref=target,
            send_sem=send_sem.at[k],
            recv_sem=recv_sem.at[k],
            device_id=device,
            device_id_type=MESH,
        )
        copy.start()
        live.append(copy)
        return copy

    def part(h):
        return pl.ds(h * half, half)

    def spot_of(slot, pz, h):
        return kv_out.at[pl.ds(((slot * 2 + core) * ZD + pz) * tiles + h * half, half)]

    def place(slot, u):
        return spot_of(slot, z_at[u[0]], u[1])

    def share(slot, u, source=None):
        shared.append(send(place(slot, u) if source is None else source, place(slot, u), partner))

    own, relayed, q_in, raw_in = {}, {}, {}, {}
    above, below, far, halo_above, halo_below, passing = {}, {}, {}, {}, {}, {}

    def send_z(h):
        own[2, h] = send(kv_ref.at[z_at[1], part(h)], spot_of(0, z, h), z_dev[1])
        own[1, h] = send(kv_ref.at[z_at[2], part(h)], spot_of(0, z, h), z_dev[2])

    def spread(u, source):
        below[u] = send(source, place(2, u), up)
        above[u] = send(source, place(1, u), down)

    def straight(u):
        passing[u] = send(place(0, u), transit.at[DIRECT.index(u)], back)

    def cross(u):
        passing[u].wait_recv()
        spot = transit.at[DIRECT.index(u)]
        halo_below[u] = send(spot, place(5, u), up)
        halo_above[u] = send(spot, place(4, u), down)

    def arrived(u, fresh=True):
        above[u].wait_recv()
        if u[1] == 1:
            far[u] = send(place(1, u), place(3, u), down)
        if fresh:
            halo_above[u] = send(place(1, u), place(4, u), halo)
        share(1, u)
        below[u].wait_recv()
        if u[1] == 0:
            far[u] = send(place(2, u), place(3, u), up)
        if fresh:
            halo_below[u] = send(place(2, u), place(5, u), halo)
        share(2, u)

    def returned(u):
        halo_above[u].wait_recv()
        above[u] = send(place(4, u), place(1, u), back)
        share(4, u)
        halo_below[u].wait_recv()
        below[u] = send(place(5, u), place(2, u), back)
        share(5, u)

    def settle(u):
        halo_above[u].wait_recv()
        share(4, u)
        halo_below[u].wait_recv()
        share(5, u)

    def settle_far(u):
        far[u].wait_recv()
        share(3, u)

    def mine(u):
        own[u].wait_recv()
        share(0, u)

    send_z(0)
    spread((0, 0), kv_ref.at[z, part(0)])
    relayed[0] = send(kv_ref.at[z_at[3], part(0)], relay.at[0], z_dev[1])
    relayed[1] = send(kv_ref.at[z_at[3], part(1)], relay.at[1], z_dev[2])
    spread((0, 1), kv_ref.at[z, part(1)])
    send_z(1)
    share(0, (0, 0), kv_ref.at[z, part(0)])
    share(0, (0, 1), kv_ref.at[z, part(1)])

    def queries(t, carry):
        q = jnp.dot(rows_of(t), wq_ref[...], preferred_element_type=jnp.float32)
        q = q.astype(jnp.bfloat16)
        for h in range(HEADS):
            q_ref[h, t] = q[:, h * HD:(h + 1) * HD]
        return carry

    loads[5].wait()
    lax.fori_loop(0, tiles, queries, 0)
    q_out[z] = q_ref[z]
    raw_all[z] = raw[...]

    mine((1, 0))
    straight((1, 0))
    mine((2, 0))
    spread((2, 0), place(0, (2, 0)))
    relayed[0].wait_recv()
    own[3, 0] = send(relay.at[0], spot_of(0, z_at[2], 0), z_dev[1])
    relayed[1].wait_recv()
    own[3, 1] = send(relay.at[1], spot_of(0, z_at[1], 1), z_dev[2])
    for j, lands in ((1, 2), (2, 1), (3, 3)):
        raw_in[lands] = send(raw, raw_all.at[z], z_dev[j])
        q_in[lands] = send(q_ref.at[z_at[j]], q_out.at[z], z_dev[j])
    arrived((0, 0))
    arrived((0, 1))
    cross((1, 0))
    mine((1, 1))
    straight((1, 1))
    mine((2, 1))
    straight((2, 1))
    arrived((2, 0))
    mine((3, 0))
    spread((3, 0), place(0, (3, 0)))
    mine((3, 1))
    spread((3, 1), place(0, (3, 1)))
    returned((1, 0))
    settle_far((0, 0))
    settle((0, 0))
    cross((1, 1))
    cross((2, 1))
    arrived((3, 0))
    arrived((3, 1))
    arrived((1, 0), fresh=False)
    settle_far((0, 1))
    settle((0, 1))
    returned((1, 1))
    returned((2, 1))

    for j in (1, 2, 3):
        raw_in[j].wait_recv()
    lists = raw_all[...].reshape(ZD * raw.shape[0], 128)

    loads[6].wait()

    def look_up(i, found):
        return jnp.where(lists == i, valid_ref[i], found)

    found = lax.fori_loop(0, valid_ref.shape[0], look_up, jnp.zeros_like(lists))
    spot = jnp.maximum(lists, 0)
    relative = (spot // 64 + 9 - zone) % 8
    there_y = (spot // 32) % 2 * 2 + 1 - y_lo
    near = jnp.where((there_y + 4 - y) % 4 == 1, 1, 2)
    near = near + jnp.where(relative == 2 - 2 * y_lo, 0, 3)
    slot = jnp.where(relative == 1, jnp.where((spot // 32) % 2 == y_hi, 0, 3), near)
    code = ((slot * 2 + (spot // 4) % 2) * ZD + (spot // 8) % ZD) * 4 + spot % 4
    code = jnp.where(lists < 0, 0, code * 256 + found)
    code = jnp.where(lane == NB, lists, code)
    for p in range(ZD):
        code_vec[p * tiles:(p + 1) * tiles, :] = code[p * raw.shape[0]:p * raw.shape[0] + tiles]

    to_smem = pltpu.make_async_copy(code_vec, code_ref, load_sem.at[11])
    to_smem.start()
    settle_far((2, 0))
    settle((2, 0))
    arrived((1, 1), fresh=False)
    arrived((2, 1), fresh=False)
    settle_far((1, 0))
    settle((3, 0))
    settle_far((3, 0))
    settle((3, 1))
    settle_far((3, 1))
    settle_far((1, 1))
    settle_far((2, 1))
    for c in shared + list(q_in.values()):
        c.wait_recv()
    to_smem.wait()

    s_bufs, p_bufs = (s_even, s_odd), (p_even, p_odd)
    d_bufs, t_bufs = (d_even, d_odd), (t_even, t_odd)
    count = ZD * tiles

    def owner(n):
        g = n // tiles
        d = jnp.where(g == 0, 2, jnp.where(g == 1, 1, jnp.where(g == 2, 3, 0)))
        return (z + d) % ZD

    def scores(n, b):
        pz, t = owner(n), n % tiles
        i = pz * tiles + t
        q = q_out[pz, t]
        top = None
        for p in range(NB // 2):
            e, f = code_ref[i, 2 * p], code_ref[i, 2 * p + 1]
            keys = jnp.concatenate([kv_out[e // 256, 0], kv_out[f // 256, 0]], axis=1)
            s = jnp.dot(q, keys, preferred_element_type=jnp.float32)
            bias = jnp.concatenate(
                [jnp.where(lane < e % 256, 0.0, NEG), jnp.where(lane < f % 256, 0.0, NEG)],
                axis=1,
            )
            s = s + bias
            s_bufs[b][:, p * 256:(p + 1) * 256] = s
            pair_top = jnp.maximum(s[:, :TILE], s[:, TILE:])
            top = pair_top if top is None else jnp.maximum(top, pair_top)
        t_bufs[b][...] = top

    def weights(b):
        for g in range(TILE // 16):
            rows = slice(g * 16, (g + 1) * 16)
            peak = jnp.max(t_bufs[b][rows, :], axis=1, keepdims=True)
            den = None
            for k in range(NB):
                cols = slice(k * TILE, (k + 1) * TILE)
                w = jnp.exp2((s_bufs[b][rows, cols] - peak) * EXP_SCALE)
                den = w if den is None else den + w
                p_bufs[b][rows, cols] = w.astype(jnp.bfloat16)
            total = jnp.sum(den, axis=1, keepdims=True)
            d_bufs[b][rows, :] = jnp.broadcast_to(1.0 / total, (16, TILE))

    def values(n, b):
        i = owner(n) * tiles + n % tiles
        v = jnp.concatenate([kv_out[code_ref[i, p] // 256, 1] for p in range(NB)], axis=0)
        acc = jnp.dot(p_bufs[b][...], v, preferred_element_type=jnp.float32)
        o_ref[n] = (acc * d_bufs[b][...]).astype(jnp.bfloat16)

    base = len(live)

    def describe(k, source, target, device):
        return pltpu.make_async_remote_copy(
            src_ref=source,
            dst_ref=target,
            send_sem=send_sem.at[base + k],
            recv_sem=recv_sem.at[base + k],
            device_id=device,
            device_id_type=MESH,
        )

    hops = [
        describe(h, o_ref.at[pl.ds(h * half, half)], hop.at[h], z_dev[1 + h]) for h in range(2)
    ]
    ends = [
        describe(2 + h, o_ref.at[pl.ds((1 + h) * tiles, tiles)], got.at[1 - h], z_dev[1 + h])
        for h in range(2)
    ]
    last = [
        describe(4 + h, hop.at[h], got.at[2, part(h)], z_dev[1 + h]) for h in range(2)
    ]

    scores(jnp.int32(0), 0)
    scores(jnp.int32(1), 1)
    weights(0)

    def pair(k, carry):
        for r in range(2):
            n = 2 * k + r
            values(n, r)
            scores(n + 2, r)
            weights(1 - r)

        @pl.when(k == 2)
        def _():
            for c in hops:
                c.start()

        @pl.when(k == 4)
        def _():
            ends[0].start()

        @pl.when(k == 5)
        def _():
            for c, d in zip(hops, last):
                c.wait_recv()
                d.start()

        @pl.when(k == 6)
        def _():
            ends[1].start()

        return carry

    lax.fori_loop(0, count // 2 - 1, pair, 0)
    values(jnp.int32(count - 2), 0)
    weights(1)
    values(jnp.int32(count - 1), 1)

    def add_head(pz, piece):
        o = piece.reshape(tiles * TILE, HD)
        w = wo_ref[pl.ds(pl.multiple_of(pz * HD, HD), HD), :]
        return jnp.dot(o, w, preferred_element_type=jnp.float32)

    for c in loads[7:]:
        c.wait()
    res_ref[...] = x_ref[...].astype(jnp.float32) + add_head(z, o_ref[3 * tiles:])
    for c in last:
        c.wait_recv()
    res_ref[...] += add_head(z_at[3], got[2])
    for h in (1, 0):
        ends[1 - h].wait_recv()
        res_ref[...] += add_head(z_at[1 + h], got[h])
    r = res_ref[...]
    inverse = lax.rsqrt(jnp.mean(r * r, axis=-1, keepdims=True) + 1e-06)
    norm_ref[...] = (r * inverse).astype(jnp.bfloat16)
    width = 256

    def hidden(f, carry):
        cols = pl.ds(pl.multiple_of(f * width, width), width)
        gate = jnp.dot(norm_ref[...], wg_ref[:, cols], preferred_element_type=jnp.float32)
        lift = jnp.dot(norm_ref[...], wu_ref[:, cols], preferred_element_type=jnp.float32)
        hid_ref[:, cols] = (gate / (1.0 + jnp.exp(-gate)) * lift).astype(jnp.bfloat16)
        return carry

    lax.fori_loop(0, wg_ref.shape[1] // width, hidden, 0)

    def lower(f, carry):
        cols = pl.ds(pl.multiple_of(f * width, width), width)
        out_ref[:, cols] = (
            res_ref[:, cols]
            + jnp.dot(hid_ref[...], wd_ref[:, cols], preferred_element_type=jnp.float32)
        ).astype(jnp.bfloat16)
        return carry

    lax.fori_loop(0, D // width, lower, 0)
    for c in live + hops + ends + last:
        c.wait_send()


def body(
    x, lists, counts, valid, w_query, w_key, w_value, w_out, w_gate, w_up, w_down
):
    tiles = x.shape[0] // TILE
    piece = (tiles, 2, TILE, HD)
    weights = (w_query, w_key, w_value, w_out, w_gate, w_up, w_down)
    copied = (x,) + weights

    def fast(shape, dtype=x.dtype):
        return pltpu.VMEM(shape, dtype)

    return pl.pallas_call(
        layer_kernel,
        out_shape=jax.ShapeDtypeStruct(x.shape, x.dtype),
        in_specs=[pl.BlockSpec(memory_space=pltpu.HBM)] * 11,
        out_specs=pl.BlockSpec(memory_space=pltpu.VMEM),
        scratch_shapes=[
            fast(lists.shape, jnp.int32),
            pltpu.SMEM(counts.shape, jnp.int32),
            pltpu.SMEM(valid.shape, jnp.int32),
        ]
        + [fast(a.shape) for a in copied]
        + [
            fast((6 * 2 * ZD * tiles,) + piece[1:]),
            fast((ZD, tiles, TILE, HD)),
            fast((HEADS,) + piece),
            fast((HEADS, tiles, TILE, HD)),
            fast((8, 128), jnp.int32),
            fast((ZD, 8, 128), jnp.int32),
            fast((2, tiles // 2) + piece[1:]),
            fast((len(DIRECT), tiles // 2) + piece[1:]),
            fast((ZD * tiles, 128), jnp.int32),
            pltpu.SMEM((ZD * tiles, 128), jnp.int32),
        ]
        + [fast((TILE, NB * TILE), jnp.float32)] * 2
        + [fast((TILE, NB * TILE))] * 2
        + [fast((TILE, TILE), jnp.float32)] * 4
        + [
            fast((ZD * tiles, TILE, HD)),
            fast((ZD - 1, tiles, TILE, HD)),
            fast((2, tiles // 2, TILE, HD)),
            fast(x.shape, jnp.float32),
            fast(x.shape),
            fast((x.shape[0], w_gate.shape[1])),
            pltpu.SemaphoreType.DMA((12,)),
            pltpu.SemaphoreType.DMA((COPIES,)),
            pltpu.SemaphoreType.DMA((COPIES,)),
        ],
        compiler_params=pltpu.CompilerParams(
            collective_id=0, has_side_effects=True, vmem_limit_bytes=67043328
        ),
    )(lists, counts, valid, x, *weights)


def solution(mesh):
    placed = (
        P(("zone", "dev"), None),
        P(("zone", "dev"), None),
        P(("zone", "dev")),
        P(),
        P(),
        P(),
        P(),
        P(),
        P(),
        P(),
        P(),
    )
    return jax.shard_map(
        body, mesh=mesh, in_specs=placed, out_specs=P(("zone", "dev"), None), check_vma=False
    )
```

time: 94.9 us -> 77.9 us (0.82)
  the two profiles are of different devices: /device:TPU:8 before, /device:TPU:1 now
where the time goes in v2:
time: 77.9 us; the launch traced here: 77.7 us
  Pallas kernels  75.8 us (97%)
  local copies, waits for them, and re-layouts  1.87 us (2%)
    pallas_call x1, Pallas kernels, body(): pl.pallas_call(layer_kernel, out_shape=jax.ShapeDtypeStruct(x.shape, x.dt...  75.8 us
    unnamed x1, local copies, waits for them, and re-layouts  1.87 us

profile of v2, /device:TPU:1, one launch (start us, length us, event | category | flops | bytes accessed | tf_op | source)
XLA Modules:
  0.0 77.7 jit_solution(9865948699994215622)
XLA Ops:
  0.0 75.8 %shard_map.109 = bf16[512,512]{1,0:T(8,128)(2,1)} custom-call(s32[4,32]{1,0:T(4,128)} %nb_hbm.1, s32[4]{0:T(128)} %count_hbm.1, s32[512]{0:T(512)} %valid_hbm.1, bf16[512,512]{1,0:T(8,128)(2,1)} %x_hbm.1, bf16[512,512]{1,0:T(8,128)(2,1)} %wq_hbm.1, bf16[512,512]{1,0:T(8,128)(2,1)} %wk_hbm.1, bf16[512,512]{1,0:T(8,128)(2,1)} %wv_hbm.1, ...), custom_call_target="tpu_custom_call" | custom-call | tf_op jit(solution)/shard_map/pallas_call | solution.py:437
  75.9 1.9 %copy.13 = bf16[512,512]{1,0:T(8,128)(2,1)} copy(bf16[512,512]{1,0:T(8,128)(2,1)} %shard_map.109) | data formatting | bytes 1048576

commit v3 on v2

--- a/solution.py
+++ b/solution.py
@@ -1,3 +1,4 @@
+import heapq
 import math
 
 import jax
@@ -18,10 +19,56 @@
 
 
 MESH = pl.DeviceIdType.MESH
-UNITS = tuple((j, h) for j in range(ZD) for h in range(2))
-DIRECT = ((1, 0), (1, 1), (2, 1))
-COPIES = 112
-ORDER = (3, 1, 2, 0)
+PARTS = 4
+DIRECT = ((1, 0), (1, 1), (1, 2), (1, 3), (2, 0), (2, 2))
+OPENING = (("own", 0), ("next", 1), ("next", 3), ("relay", 1), ("next", 2), ("relay", 2), ("own", 3), ("own", 2), ("next", 0), ("relay", 3), ("own", 1), ("relay", 0))
+FAR_UP = ((0, 0), (1, 0), (1, 2), (2, 0), (2, 3), (3, 0), (3, 1), (3, 3))
+
+
+COPIES = 210
+
+
+def arrivals():
+    unit, hop = 5.6 / PARTS, 3.1
+    free, events, order = {}, [], []
+
+    def send(now, key, link):
+        free[link] = max(now, free.get(link, 0.0)) + unit
+        heapq.heappush(events, (free[link] + hop, len(order) + len(events), key))
+
+    def own(now, u):
+        if u in DIRECT:
+            send(now, ("transit", u), "back")
+        else:
+            send(now, ("below", u), "up")
+            send(now, ("above", u), "down")
+
+    for kind, h in OPENING:
+        if kind == "own":
+            own(0.0, (0, h))
+        elif kind == "next":
+            send(0.0, ("own", (2, h)), "next")
+            send(0.0, ("own", (1, h)), "prior")
+        else:
+            send(0.0, ("relay", h), "next" if 2 * h < PARTS else "prior")
+    while events:
+        now, _, (kind, u) = heapq.heappop(events)
+        order.append((kind, u))
+        if kind == "own":
+            own(now, u)
+        elif kind == "relay":
+            send(now, ("own", (3, u)), "next" if 2 * u < PARTS else "prior")
+        elif kind == "transit":
+            send(now, ("halo_below", u), "up")
+            send(now, ("halo_above", u), "down")
+        elif kind in ("above", "below"):
+            if (kind == "below") == (u in FAR_UP):
+                send(now, ("far", u), "up" if kind == "below" else "down")
+            if u not in DIRECT:
+                send(now, ("halo_" + kind, u), "halo")
+        elif kind in ("halo_above", "halo_below") and u in DIRECT:
+            send(now, (kind[5:], u), "back")
+    return order
 
 
 def layer_kernel(
@@ -38,6 +85,7 @@
     y_hi, z, core = dev // 8, (dev // 2) % ZD, dev % 2
     y = y_hi * 2 + y_lo
     tiles = x_ref.shape[0] // TILE
+    size = tiles // PARTS
     half = tiles // 2
 
     def at(px, py, pz, pc):
@@ -95,7 +143,7 @@
     kv_out[pl.ds((core * ZD + z) * tiles, tiles)] = kv_ref[z]
     pl.semaphore_wait(barrier, len(peers))
 
-    live, shared = [], []
+    live, flying, shared = [], {}, []
 
     def send(source, target, device):
         k = len(live)
@@ -112,10 +160,10 @@
         return copy
 
     def part(h):
-        return pl.ds(h * half, half)
+        return pl.ds(h * size, size)
 
     def spot_of(slot, pz, h):
-        return kv_out.at[pl.ds(((slot * 2 + core) * ZD + pz) * tiles + h * half, half)]
+        return kv_out.at[pl.ds(((slot * 2 + core) * ZD + pz) * tiles + h * size, size)]
 
     def place(slot, u):
         return spot_of(slot, z_at[u[0]], u[1])
@@ -123,70 +171,58 @@
     def share(slot, u, source=None):
         shared.append(send(place(slot, u) if source is None else source, place(slot, u), partner))
 
-    own, relayed, q_in, raw_in = {}, {}, {}, {}
-    above, below, far, halo_above, halo_below, passing = {}, {}, {}, {}, {}, {}
-
-    def send_z(h):
-        own[2, h] = send(kv_ref.at[z_at[1], part(h)], spot_of(0, z, h), z_dev[1])
-        own[1, h] = send(kv_ref.at[z_at[2], part(h)], spot_of(0, z, h), z_dev[2])
-
-    def spread(u, source):
-        below[u] = send(source, place(2, u), up)
-        above[u] = send(source, place(1, u), down)
-
-    def straight(u):
-        passing[u] = send(place(0, u), transit.at[DIRECT.index(u)], back)
-
-    def cross(u):
-        passing[u].wait_recv()
-        spot = transit.at[DIRECT.index(u)]
-        halo_below[u] = send(spot, place(5, u), up)
-        halo_above[u] = send(spot, place(4, u), down)
-
-    def arrived(u, fresh=True):
-        above[u].wait_recv()
-        if u[1] == 1:
-            far[u] = send(place(1, u), place(3, u), down)
-        if fresh:
-            halo_above[u] = send(place(1, u), place(4, u), halo)
-        share(1, u)
-        below[u].wait_recv()
-        if u[1] == 0:
-            far[u] = send(place(2, u), place(3, u), up)
-        if fresh:
-            halo_below[u] = send(place(2, u), place(5, u), halo)
-        share(2, u)
-
-    def returned(u):
-        halo_above[u].wait_recv()
-        above[u] = send(place(4, u), place(1, u), back)
-        share(4, u)
-        halo_below[u].wait_recv()
-        below[u] = send(place(5, u), place(2, u), back)
-        share(5, u)
-
-    def settle(u):
-        halo_above[u].wait_recv()
-        share(4, u)
-        halo_below[u].wait_recv()
-        share(5, u)
-
-    def settle_far(u):
-        far[u].wait_recv()
-        share(3, u)
-
-    def mine(u):
-        own[u].wait_recv()
-        share(0, u)
-
-    send_z(0)
-    spread((0, 0), kv_ref.at[z, part(0)])
-    relayed[0] = send(kv_ref.at[z_at[3], part(0)], relay.at[0], z_dev[1])
-    relayed[1] = send(kv_ref.at[z_at[3], part(1)], relay.at[1], z_dev[2])
-    spread((0, 1), kv_ref.at[z, part(1)])
-    send_z(1)
-    share(0, (0, 0), kv_ref.at[z, part(0)])
-    share(0, (0, 1), kv_ref.at[z, part(1)])
+    def own(u, source):
+        if u in DIRECT:
+            flying["transit", u] = send(source, transit.at[DIRECT.index(u)], back)
+        else:
+            flying["below", u] = send(source, place(2, u), up)
+            flying["above", u] = send(source, place(1, u), down)
+        share(0, u, source)
+
+    def forward(kind, u):
+        flying[kind, u].wait_recv()
+        if kind == "own":
+            own(u, place(0, u))
+        elif kind == "relay":
+            along = 2 * u < PARTS
+            flying["own", (3, u)] = send(
+                relay.at[u], spot_of(0, z_at[2 if along else 1], u), z_dev[1 if along else 2]
+            )
+        elif kind == "transit":
+            spot = transit.at[DIRECT.index(u)]
+            flying["halo_below", u] = send(spot, place(5, u), up)
+            flying["halo_above", u] = send(spot, place(4, u), down)
+        elif kind in ("above", "below"):
+            slot = 1 if kind == "above" else 2
+            if (kind == "below") == (u in FAR_UP):
+                flying["far", u] = send(
+                    place(slot, u), place(3, u), up if kind == "below" else down
+                )
+            if u not in DIRECT:
+                flying["halo_" + kind, u] = send(place(slot, u), place(slot + 3, u), halo)
+            share(slot, u)
+        elif kind == "far":
+            share(3, u)
+        else:
+            slot = 4 if kind == "halo_above" else 5
+            if u in DIRECT:
+                flying[kind[5:], u] = send(place(slot, u), place(slot - 3, u), back)
+            share(slot, u)
+
+    for kind, h in OPENING:
+        if kind == "own":
+            own((0, h), kv_ref.at[z, part(h)])
+        elif kind == "next":
+            flying["own", (2, h)] = send(
+                kv_ref.at[z_at[1], part(h)], spot_of(0, z, h), z_dev[1]
+            )
+            flying["own", (1, h)] = send(
+                kv_ref.at[z_at[2], part(h)], spot_of(0, z, h), z_dev[2]
+            )
+        else:
+            flying["relay", h] = send(
+                kv_ref.at[z_at[3], part(h)], relay.at[h], z_dev[1 if 2 * h < PARTS else 2]
+            )
 
     def queries(t, carry):
         q = jnp.dot(rows_of(t), wq_ref[...], preferred_element_type=jnp.float32)
@@ -200,41 +236,17 @@
     q_out[z] = q_ref[z]
     raw_all[z] = raw[...]
 
-    mine((1, 0))
-    straight((1, 0))
-    mine((2, 0))
-    spread((2, 0), place(0, (2, 0)))
-    relayed[0].wait_recv()
-    own[3, 0] = send(relay.at[0], spot_of(0, z_at[2], 0), z_dev[1])
-    relayed[1].wait_recv()
-    own[3, 1] = send(relay.at[1], spot_of(0, z_at[1], 1), z_dev[2])
+    order = arrivals()
+    relays = [n for n, (kind, _) in enumerate(order) if kind == "relay"]
+    middle = 2 * len(order) // 3
+    for kind, u in order[:relays[-1] + 1]:
+        forward(kind, u)
+    q_in, raw_in = {}, {}
     for j, lands in ((1, 2), (2, 1), (3, 3)):
         raw_in[lands] = send(raw, raw_all.at[z], z_dev[j])
         q_in[lands] = send(q_ref.at[z_at[j]], q_out.at[z], z_dev[j])
-    arrived((0, 0))
-    arrived((0, 1))
-    cross((1, 0))
-    mine((1, 1))
-    straight((1, 1))
-    mine((2, 1))
-    straight((2, 1))
-    arrived((2, 0))
-    mine((3, 0))
-    spread((3, 0), place(0, (3, 0)))
-    mine((3, 1))
-    spread((3, 1), place(0, (3, 1)))
-    returned((1, 0))
-    settle_far((0, 0))
-    settle((0, 0))
-    cross((1, 1))
-    cross((2, 1))
-    arrived((3, 0))
-    arrived((3, 1))
-    arrived((1, 0), fresh=False)
-    settle_far((0, 1))
-    settle((0, 1))
-    returned((1, 1))
-    returned((2, 1))
+    for kind, u in order[relays[-1] + 1:middle]:
+        forward(kind, u)
 
     for j in (1, 2, 3):
         raw_in[j].wait_recv()
@@ -242,10 +254,13 @@
 
     loads[6].wait()
 
+    span = 3 * 64
+
     def look_up(i, found):
-        return jnp.where(lists == i, valid_ref[i], found)
-
-    found = lax.fori_loop(0, valid_ref.shape[0], look_up, jnp.zeros_like(lists))
+        g = (zone * 64 + valid_ref.shape[0] - 64 + i) % valid_ref.shape[0]
+        return jnp.where(lists == g, valid_ref[g], found)
+
+    found = lax.fori_loop(0, span, look_up, jnp.zeros_like(lists), unroll=8)
     spot = jnp.maximum(lists, 0)
     relative = (spot // 64 + 9 - zone) % 8
     there_y = (spot // 32) % 2 * 2 + 1 - y_lo
@@ -260,17 +275,8 @@
 
     to_smem = pltpu.make_async_copy(code_vec, code_ref, load_sem.at[11])
     to_smem.start()
-    settle_far((2, 0))
-    settle((2, 0))
-    arrived((1, 1), fresh=False)
-    arrived((2, 1), fresh=False)
-    settle_far((1, 0))
-    settle((3, 0))
-    settle_far((3, 0))
-    settle((3, 1))
-    settle_far((3, 1))
-    settle_far((1, 1))
-    settle_far((2, 1))
+    for kind, u in order[middle:]:
+        forward(kind, u)
     for c in shared + list(q_in.values()):
         c.wait_recv()
     to_smem.wait()
@@ -342,7 +348,7 @@
         for h in range(2)
     ]
     last = [
-        describe(4 + h, hop.at[h], got.at[2, part(h)], z_dev[1 + h]) for h in range(2)
+        describe(4 + h, hop.at[h], got.at[2, pl.ds(h * half, half)], z_dev[1 + h]) for h in range(2)
     ]
 
     scores(jnp.int32(0), 0)
@@ -452,8 +458,8 @@
             fast((HEADS, tiles, TILE, HD)),
             fast((8, 128), jnp.int32),
             fast((ZD, 8, 128), jnp.int32),
-            fast((2, tiles // 2) + piece[1:]),
-            fast((len(DIRECT), tiles // 2) + piece[1:]),
+            fast((PARTS, tiles // PARTS) + piece[1:]),
+            fast((len(DIRECT), tiles // PARTS) + piece[1:]),
             fast((ZD * tiles, 128), jnp.int32),
             pltpu.SMEM((ZD * tiles, 128), jnp.int32),
         ]

time: 77.9 us -> 75.9 us (0.974)
  Pallas kernels: 75.8 us -> 73.9 us
    pallas_call x1, Pallas kernels: 75.8 us -> 73.9 us  [body(): pl.pallas_call(layer_kernel, out_shape=jax.ShapeDtypeStruct(x.shape, x.dt...]
where the time goes in v3:
time: 75.9 us; the launch traced here: 75.8 us
  Pallas kernels  73.9 us (97%)
  local copies, waits for them, and re-layouts  1.87 us (2%)
    pallas_call x1, Pallas kernels, body(): pl.pallas_call(layer_kernel, out_shape=jax.ShapeDtypeStruct(x.shape, x.dt...  73.9 us
    unnamed x1, local copies, waits for them, and re-layouts  1.87 us

profile of v3, /device:TPU:1, one launch (start us, length us, event | category | flops | bytes accessed | tf_op | source)
XLA Modules:
  0.0 75.8 jit_solution(13341511429670370830)
XLA Ops:
  0.0 73.9 %shard_map.109 = bf16[512,512]{1,0:T(8,128)(2,1)} custom-call(s32[4,32]{1,0:T(4,128)} %nb_hbm.1, s32[4]{0:T(128)} %count_hbm.1, s32[512]{0:T(512)} %valid_hbm.1, bf16[512,512]{1,0:T(8,128)(2,1)} %x_hbm.1, bf16[512,512]{1,0:T(8,128)(2,1)} %wq_hbm.1, bf16[512,512]{1,0:T(8,128)(2,1)} %wk_hbm.1, bf16[512,512]{1,0:T(8,128)(2,1)} %wv_hbm.1, ...), custom_call_target="tpu_custom_call" | custom-call | tf_op jit(solution)/shard_map/pallas_call | solution.py:443
  73.9 1.9 %copy.13 = bf16[512,512]{1,0:T(8,128)(2,1)} copy(bf16[512,512]{1,0:T(8,128)(2,1)} %shard_map.109) | data formatting | bytes 1048576

commit v4 on v3

--- a/solution.py
+++ b/solution.py
@@ -76,7 +76,7 @@
     out_ref,
     nb_ref, count_ref, valid_ref, x_ref, wq_ref, wk_ref, wv_ref, wo_ref, wg_ref, wu_ref, wd_ref,
     kv_out, q_out, kv_ref, q_ref, raw, raw_all, relay, transit, code_vec, code_ref,
-    s_even, s_odd, p_even, p_odd, d_even, d_odd, t_even, t_odd,
+    s_even, s_odd, p_even, p_odd, t_even, t_odd,
     o_ref, got, hop, res_ref, norm_ref, hid_ref,
     load_sem, send_sem, recv_sem,
 ):
@@ -282,7 +282,7 @@
     to_smem.wait()
 
     s_bufs, p_bufs = (s_even, s_odd), (p_even, p_odd)
-    d_bufs, t_bufs = (d_even, d_odd), (t_even, t_odd)
+    t_bufs = (t_even, t_odd)
     count = ZD * tiles
 
     def owner(n):
@@ -313,20 +313,25 @@
         for g in range(TILE // 16):
             rows = slice(g * 16, (g + 1) * 16)
             peak = jnp.max(t_bufs[b][rows, :], axis=1, keepdims=True)
-            den = None
             for k in range(NB):
                 cols = slice(k * TILE, (k + 1) * TILE)
                 w = jnp.exp2((s_bufs[b][rows, cols] - peak) * EXP_SCALE)
-                den = w if den is None else den + w
                 p_bufs[b][rows, cols] = w.astype(jnp.bfloat16)
-            total = jnp.sum(den, axis=1, keepdims=True)
-            d_bufs[b][rows, :] = jnp.broadcast_to(1.0 / total, (16, TILE))
 
     def values(n, b):
         i = owner(n) * tiles + n % tiles
-        v = jnp.concatenate([kv_out[code_ref[i, p] // 256, 1] for p in range(NB)], axis=0)
-        acc = jnp.dot(p_bufs[b][...], v, preferred_element_type=jnp.float32)
-        o_ref[n] = (acc * d_bufs[b][...]).astype(jnp.bfloat16)
+        ones = jnp.ones((2 * TILE, TILE), jnp.bfloat16)
+        acc = None
+        for p in range(NB // 2):
+            e, f = code_ref[i, 2 * p], code_ref[i, 2 * p + 1]
+            v = jnp.concatenate([kv_out[e // 256, 1], kv_out[f // 256, 1]], axis=0)
+            share_p = jnp.dot(
+                p_bufs[b][:, p * 256:(p + 1) * 256],
+                jnp.concatenate([v, ones], axis=1),
+                preferred_element_type=jnp.float32,
+            )
+            acc = share_p if acc is None else acc + share_p
+        o_ref[n] = (acc[:, :HD] / acc[:, HD:]).astype(jnp.bfloat16)
 
     base = len(live)
 
@@ -406,15 +411,16 @@
     inverse = lax.rsqrt(jnp.mean(r * r, axis=-1, keepdims=True) + 1e-06)
     norm_ref[...] = (r * inverse).astype(jnp.bfloat16)
     width = 256
+    broad = 512
 
     def hidden(f, carry):
-        cols = pl.ds(pl.multiple_of(f * width, width), width)
+        cols = pl.ds(pl.multiple_of(f * broad, broad), broad)
         gate = jnp.dot(norm_ref[...], wg_ref[:, cols], preferred_element_type=jnp.float32)
         lift = jnp.dot(norm_ref[...], wu_ref[:, cols], preferred_element_type=jnp.float32)
         hid_ref[:, cols] = (gate / (1.0 + jnp.exp(-gate)) * lift).astype(jnp.bfloat16)
         return carry
 
-    lax.fori_loop(0, wg_ref.shape[1] // width, hidden, 0)
+    lax.fori_loop(0, wg_ref.shape[1] // broad, hidden, 0)
 
     def lower(f, carry):
         cols = pl.ds(pl.multiple_of(f * width, width), width)
@@ -465,7 +471,7 @@
         ]
         + [fast((TILE, NB * TILE), jnp.float32)] * 2
         + [fast((TILE, NB * TILE))] * 2
-        + [fast((TILE, TILE), jnp.float32)] * 4
+        + [fast((TILE, TILE), jnp.float32)] * 2
         + [
             fast((ZD * tiles, TILE, HD)),
             fast((ZD - 1, tiles, TILE, HD)),

time: 75.9 us -> 73.6 us (0.970)
  Pallas kernels: 73.9 us -> 71.5 us
    pallas_call x1, Pallas kernels: 73.9 us -> 71.5 us  [body(): pl.pallas_call(layer_kernel, out_shape=jax.ShapeDtypeStruct(x.shape, x.dt...]
where the time goes in v4:
time: 73.6 us; the launch traced here: 73.4 us
  Pallas kernels  71.5 us (97%)
  local copies, waits for them, and re-layouts  1.87 us (3%)
    pallas_call x1, Pallas kernels, body(): pl.pallas_call(layer_kernel, out_shape=jax.ShapeDtypeStruct(x.shape, x.dt...  71.5 us
    unnamed x1, local copies, waits for them, and re-layouts  1.87 us

profile of v4, /device:TPU:1, one launch (start us, length us, event | category | flops | bytes accessed | tf_op | source)
XLA Modules:
  0.0 73.4 jit_solution(7309465917459027839)
XLA Ops:
  0.0 71.5 %shard_map.109 = bf16[512,512]{1,0:T(8,128)(2,1)} custom-call(s32[4,32]{1,0:T(4,128)} %nb_hbm.1, s32[4]{0:T(128)} %count_hbm.1, s32[512]{0:T(512)} %valid_hbm.1, bf16[512,512]{1,0:T(8,128)(2,1)} %x_hbm.1, bf16[512,512]{1,0:T(8,128)(2,1)} %wq_hbm.1, bf16[512,512]{1,0:T(8,128)(2,1)} %wk_hbm.1, bf16[512,512]{1,0:T(8,128)(2,1)} %wv_hbm.1, ...), custom_call_target="tpu_custom_call" | custom-call | tf_op jit(solution)/shard_map/pallas_call | solution.py:449
  71.5 1.9 %copy.13 = bf16[512,512]{1,0:T(8,128)(2,1)} copy(bf16[512,512]{1,0:T(8,128)(2,1)} %shard_map.109) | data formatting | bytes 1048576

commit v5 on v4

--- a/solution.py
+++ b/solution.py
@@ -77,7 +77,7 @@
     nb_ref, count_ref, valid_ref, x_ref, wq_ref, wk_ref, wv_ref, wo_ref, wg_ref, wu_ref, wd_ref,
     kv_out, q_out, kv_ref, q_ref, raw, raw_all, relay, transit, code_vec, code_ref,
     s_even, s_odd, p_even, p_odd, t_even, t_odd,
-    o_ref, got, hop, res_ref, norm_ref, hid_ref,
+    o_ref, seen, got, hop, res_ref, norm_ref, hid_ref,
     load_sem, send_sem, recv_sem,
 ):
     zone, dev = lax.axis_index("zone"), lax.axis_index("dev")
@@ -367,22 +367,34 @@
             scores(n + 2, r)
             weights(1 - r)
 
-        @pl.when(k == 2)
+        @pl.when(k == 1)
+        def _():
+            seen[...] = o_ref[2:4]
+
+        @pl.when(k == 1)
         def _():
             for c in hops:
                 c.start()
 
+        @pl.when(k == 3)
+        def _():
+            seen[...] = o_ref[6:8]
+
+        @pl.when(k == 3)
+        def _():
+            ends[0].start()
+
         @pl.when(k == 4)
-        def _():
-            ends[0].start()
-
-        @pl.when(k == 5)
         def _():
             for c, d in zip(hops, last):
                 c.wait_recv()
                 d.start()
 
-        @pl.when(k == 6)
+        @pl.when(k == 5)
+        def _():
+            seen[...] = o_ref[10:12]
+
+        @pl.when(k == 5)
         def _():
             ends[1].start()
 
@@ -474,6 +486,7 @@
         + [fast((TILE, TILE), jnp.float32)] * 2
         + [
             fast((ZD * tiles, TILE, HD)),
+            fast((2, TILE, HD)),
             fast((ZD - 1, tiles, TILE, HD)),
             fast((2, tiles // 2, TILE, HD)),
             fast(x.shape, jnp.float32),

time: 73.6 us -> 71.9 us (0.977)
  Pallas kernels: 71.5 us -> 69.9 us
    pallas_call x1, Pallas kernels: 71.5 us -> 69.9 us  [body(): pl.pallas_call(layer_kernel, out_shape=jax.ShapeDtypeStruct(x.shape, x.dt...]
where the time goes in v5:
time: 71.9 us; the launch traced here: 71.7 us
  Pallas kernels  69.9 us (97%)
  local copies, waits for them, and re-layouts  1.87 us (3%)
    pallas_call x1, Pallas kernels, body(): pl.pallas_call(layer_kernel, out_shape=jax.ShapeDtypeStruct(x.shape, x.dt...  69.9 us
    unnamed x1, local copies, waits for them, and re-layouts  1.87 us

profile of v5, /device:TPU:1, one launch (start us, length us, event | category | flops | bytes accessed | tf_op | source)
XLA Modules:
  0.0 71.7 jit_solution(3296542458985677654)
XLA Ops:
  0.0 69.9 %shard_map.109 = bf16[512,512]{1,0:T(8,128)(2,1)} custom-call(s32[4,32]{1,0:T(4,128)} %nb_hbm.1, s32[4]{0:T(128)} %count_hbm.1, s32[512]{0:T(512)} %valid_hbm.1, bf16[512,512]{1,0:T(8,128)(2,1)} %x_hbm.1, bf16[512,512]{1,0:T(8,128)(2,1)} %wq_hbm.1, bf16[512,512]{1,0:T(8,128)(2,1)} %wk_hbm.1, bf16[512,512]{1,0:T(8,128)(2,1)} %wv_hbm.1, ...), custom_call_target="tpu_custom_call" | custom-call | tf_op jit(solution)/shard_map/pallas_call | solution.py:461
  69.9 1.9 %copy.13 = bf16[512,512]{1,0:T(8,128)(2,1)} copy(bf16[512,512]{1,0:T(8,128)(2,1)} %shard_map.109) | data formatting | bytes 1048576

commit v6 on v5

--- a/solution.py
+++ b/solution.py
@@ -25,7 +25,7 @@
 FAR_UP = ((0, 0), (1, 0), (1, 2), (2, 0), (2, 3), (3, 0), (3, 1), (3, 3))
 
 
-COPIES = 210
+COPIES = 212
 
 
 def arrivals():
@@ -349,8 +349,9 @@
         describe(h, o_ref.at[pl.ds(h * half, half)], hop.at[h], z_dev[1 + h]) for h in range(2)
     ]
     ends = [
-        describe(2 + h, o_ref.at[pl.ds((1 + h) * tiles, tiles)], got.at[1 - h], z_dev[1 + h])
-        for h in range(2)
+        describe(2, o_ref.at[pl.ds(tiles, tiles)], got.at[1], z_dev[1]),
+        describe(3, o_ref.at[pl.ds(2 * tiles, half)], got.at[0, pl.ds(0, half)], z_dev[2]),
+        describe(6, o_ref.at[pl.ds(2 * tiles + half, half)], got.at[0, pl.ds(half, half)], z_dev[2]),
     ]
     last = [
         describe(4 + h, hop.at[h], got.at[2, pl.ds(h * half, half)], z_dev[1 + h]) for h in range(2)
@@ -389,6 +390,11 @@
             for c, d in zip(hops, last):
                 c.wait_recv()
                 d.start()
+            seen[...] = o_ref[8:10]
+
+        @pl.when(k == 4)
+        def _():
+            ends[1].start()
 
         @pl.when(k == 5)
         def _():
@@ -396,7 +402,7 @@
 
         @pl.when(k == 5)
         def _():
-            ends[1].start()
+            ends[2].start()
 
         return carry
 
@@ -416,9 +422,11 @@
     for c in last:
         c.wait_recv()
     res_ref[...] += add_head(z_at[3], got[2])
-    for h in (1, 0):
-        ends[1 - h].wait_recv()
-        res_ref[...] += add_head(z_at[1 + h], got[h])
+    ends[0].wait_recv()
+    res_ref[...] += add_head(z_at[2], got[1])
+    ends[1].wait_recv()
+    ends[2].wait_recv()
+    res_ref[...] += add_head(z_at[1], got[0])
     r = res_ref[...]
     inverse = lax.rsqrt(jnp.mean(r * r, axis=-1, keepdims=True) + 1e-06)
     norm_ref[...] = (r * inverse).astype(jnp.bfloat16)

time: 71.9 us -> 71.9 us (level)
  no operation moved by 1% of the time
where the time goes in v6:
time: 71.9 us; the launch traced here: 71.8 us
  Pallas kernels  69.9 us (97%)
  local copies, waits for them, and re-layouts  1.87 us (3%)
    pallas_call x1, Pallas kernels, body(): pl.pallas_call(layer_kernel, out_shape=jax.ShapeDtypeStruct(x.shape, x.dt...  69.9 us
    unnamed x1, local copies, waits for them, and re-layouts  1.87 us

profile of v6, /device:TPU:1, one launch (start us, length us, event | category | flops | bytes accessed | tf_op | source)
XLA Modules:
  0.0 71.8 jit_solution(10644857262633239679)
XLA Ops:
  0.0 69.9 %shard_map.109 = bf16[512,512]{1,0:T(8,128)(2,1)} custom-call(s32[4,32]{1,0:T(4,128)} %nb_hbm.1, s32[4]{0:T(128)} %count_hbm.1, s32[512]{0:T(512)} %valid_hbm.1, bf16[512,512]{1,0:T(8,128)(2,1)} %x_hbm.1, bf16[512,512]{1,0:T(8,128)(2,1)} %wq_hbm.1, bf16[512,512]{1,0:T(8,128)(2,1)} %wk_hbm.1, bf16[512,512]{1,0:T(8,128)(2,1)} %wv_hbm.1, ...), custom_call_target="tpu_custom_call" | custom-call | tf_op jit(solution)/shard_map/pallas_call | solution.py:469
  69.9 1.9 %copy.13 = bf16[512,512]{1,0:T(8,128)(2,1)} copy(bf16[512,512]{1,0:T(8,128)(2,1)} %shard_map.109) | data formatting | bytes 1048576
